TPU v7x, 256 devices: a whole 4x4x8 slice. The times are simulated.
256 devices in a mesh: row: 16 (over y_lo, x, core), col: 16 (over z, y_hi).
Axes of the slice: x: 4, y: 4 (y_hi: 2, y_lo: 2; y = y_hi * 2 + y_lo), z: 8, core: 2. Of those that a mesh axis runs over, the one named last changes fastest.
Arguments:
- collocation: bfloat16 [32768, 2048], P('col', 'row'), may hold values from -6 to 6
- greens: bfloat16 [2, 256, 2048], P(None, None, 'row'), may hold values from -0.0078125 to 0.0078125
- trial_orbitals: bfloat16 [256, 2048], P(None, 'row'), may hold values from -0.125 to 0.125
- coulomb: bfloat16 [16, 2048, 32768], P(None, 'row', 'col'), may hold values from -0.03125 to 0.03125
Outputs:
- gradient: bfloat16 [256, 2, 2048], P('col', None, 'row')
All inputs are finite; a program needn't handle non-finite values.
Results may differ from a plain program's by a relative error of at most 0.039.
Values may be sent and summed in bfloat16 or wider, within the bound.
No kernel may reach another device: no remote copies, remote signals or barrier semaphores. Data moves between devices by JAX's collectives and lax.ppermute only.
A program may use at most 64 MiB of HBM per device.

v0:
```python
import math

import jax
import jax.numpy as jnp
from jax import lax
from jax.sharding import Mesh
from jax.sharding import PartitionSpec as P

P_SIZE = 32768
COL = ("col_0", "col_1")


def split_up(shard, dim, devices):
    dims = shard.shape
    blocks = shard.reshape(*dims[:dim], devices, dims[dim] // devices, *dims[dim + 1 :])
    return jnp.moveaxis(blocks, dim, 0)


def summed_on_arrival(shard, axis, dim):
    devices = lax.axis_size(axis)
    blocks = lax.all_to_all(split_up(shard, dim, devices), axis, 0, 0, tiled=True)
    return jnp.sum(blocks.astype(jnp.float32), axis=0)


def copy_for_each(shard, axis):
    devices = lax.axis_size(axis)
    return lax.all_to_all(
        jnp.broadcast_to(shard[None], (devices, *shard.shape)), axis, 0, 0, tiled=True
    )


def laid_out(blocks, dim):
    dims = list(blocks.shape[1:])
    dims[dim] *= blocks.shape[0]
    return jnp.moveaxis(blocks, 0, dim).reshape(dims)


def collect(shard, axis, dim):
    blocks = copy_for_each(shard, axis)
    return laid_out(blocks, dim)


def gather_axes(shard, axes, dim):
    out = shard
    for number in range(len(axes) - 1, -1, -1):
        out = lax.all_gather(out, axes[number], axis=dim, tiled=True)
    return out


def in_one_piece(arrays, axis, dim, along):
    widths = [a.shape[along] for a in arrays]
    both = jnp.concatenate(arrays, axis=along)
    out = lax.psum_scatter(both, axis, scatter_dimension=dim, tiled=True)
    return tuple(jnp.split(out, [sum(widths[:k]) for k in range(1, len(widths))], axis=along))


def make_forces(exchange_sum, potential, orbit_part, walkers, occupied):
    orbit_wide = orbit_part.astype(jnp.float32)
    pieces = []
    for walker in range(walkers):
        pieces.append(
            potential[:, walker : walker + 1] * orbit_wide
            - exchange_sum[:, walker * occupied : (walker + 1) * occupied]
        )
    return jnp.concatenate(pieces, axis=1).astype(jnp.bfloat16)


def on_device(collocation, greens, trial_orbitals, coulomb):
    walkers, occupied, basis_local = greens.shape
    stacked = jnp.concatenate([trial_orbitals[None], greens], axis=0).reshape(
        (walkers + 1) * occupied, basis_local
    )
    partial_value = jnp.einsum(
        "pm,km->pk", collocation, stacked, preferred_element_type=jnp.float32
    )
    own_points = summed_on_arrival(partial_value.astype(jnp.bfloat16), "row", 0).astype(
        jnp.bfloat16
    )
    col_orbitals = collect(own_points[:, :occupied], "row", 0)
    kernel_rows = coulomb.reshape(coulomb.shape[0] * coulomb.shape[1], coulomb.shape[2])
    col_count = kernel_rows.shape[1]
    start_totals = (
        jnp.zeros((col_count, walkers * occupied), jnp.float32),
        jnp.zeros((col_count, walkers), jnp.float32),
    )
    shard_rows = gather_axes(own_points, COL, 0)
    height = shard_rows.shape[0]
    step_rows = math.gcd(height, 512)

    def advance(turn, inner):
        k_total, u_total = inner
        block_rows = lax.dynamic_slice_in_dim(shard_rows, turn * step_rows, step_rows, 0)
        v_rows = lax.dynamic_slice_in_dim(kernel_rows, turn * step_rows, step_rows, 0)
        x_rows = block_rows[:, :occupied]
        k_parts = []
        u_parts = []
        for walker in range(walkers):
            theta_rows = block_rows[:, (walker + 1) * occupied : (walker + 2) * occupied]
            t_tile = jnp.einsum(
                "pi,qi->pq", theta_rows, col_orbitals, preferred_element_type=jnp.float32
            )
            amplitude = (v_rows * t_tile).astype(jnp.bfloat16)
            k_parts.append(
                jnp.einsum("pq,pi->qi", amplitude, x_rows, preferred_element_type=jnp.float32)
            )
            density = jnp.sum(
                x_rows.astype(jnp.float32) * theta_rows.astype(jnp.float32), axis=1
            ).astype(jnp.bfloat16)
            u_parts.append(
                jnp.einsum("p,pq->q", density, v_rows, preferred_element_type=jnp.float32)
            )
        return (k_total + jnp.concatenate(k_parts, axis=1), u_total + jnp.stack(u_parts, axis=1))

    k_total, u_total = lax.fori_loop(0, height // step_rows, advance, start_totals)
    k_share, u_share = tuple(
        (
            part.astype(jnp.float32)
            for part in in_one_piece(
                (k_total.astype(jnp.bfloat16), u_total.astype(jnp.bfloat16)), "row", 0, 1
            )
        )
    )
    force_share = make_forces(k_share, u_share, own_points[:, :occupied], walkers, occupied)
    forces = collect(force_share, "row", 0)
    width_rows = occupied // lax.axis_size(COL) * lax.axis_size(COL)
    terms = []
    for walker in range(walkers):
        force_cols = lax.dynamic_slice_in_dim(forces, walker * occupied, width_rows, 1)
        terms.append(
            jnp.einsum("qi,qm->im", force_cols, collocation, preferred_element_type=jnp.float32)
        )
    gradient = summed_on_arrival(jnp.stack(terms, axis=1).astype(jnp.bfloat16), COL, 0)
    return (gradient * P_SIZE ** (-0.5)).astype(jnp.bfloat16)


def solution(mesh):
    finer = Mesh(mesh.devices.reshape(mesh.shape["row"], 8, 2), ("row", "col_0", "col_1"))
    placed = (P(COL, "row"), P(None, None, "row"), P(None, "row"), P(None, "row", COL))
    return jax.shard_map(
        on_device, mesh=finer, in_specs=placed, out_specs=P(COL, None, "row"), check_vma=False
    )
```

profile of v0, /device:TPU:1, one launch (start us, length us, event | category | flops | bytes accessed | tf_op | source)
XLA Modules:
  0.0 331.1 jit_solution(7155311509721410960)
XLA Ops:
  6.5 1.0 pad_maximum_fusion.1
  7.7 1.0 fusion.14
  8.7 0.8 copy.27
  9.5 44.3 %all_to_all.20 = bf16[16,128,768]{1,2,0:T(8,128)(2,1)} all-to-all(bf16[16,128,768]{1,2,0:T(8,128)(2,1)S(1)} %bitcast.55), channel_id=1, replica_groups=mesh['row'=16,'col_0'=8,'col_1'=2] {'row'}, dimensions={0} | all-to-all | bytes 6291456 | tf_op jit(solution)/shard_map/all_to_all | solution.py:21
  53.8 2.4 reduce_sum.47
  56.1 7.3 %all_gather.6 = bf16[256,768]{0,1:T(8,128)(2,1)} all-gather(bf16[128,768]{0,1:T(8,128)(2,1)S(1)} %reduce_sum.47), channel_id=1, replica_groups=mesh['row'=16,'col_0'=8,'col_1'=2] {'col_1'}, dimensions={0}, use_global_device_ids=true | all-gather | bytes 589824 | tf_op jit(solution)/shard_map/all_gather | solution.py:46
  63.6 1.1 broadcast_in_dim.24
  64.7 6.4 %all-to-all-start.1 = ((bf16[16,128,256]{2,1,0:T(8,128)(2,1)}), bf16[16,128,256]{2,1,0:T(8,128)(2,1)}, u32[]{:S(2)}, u32[]{:S(2)}) async-start(bf16[16,128,256]{2,1,0:T(8,128)(2,1)} %broadcast_in_dim.24), calls=%async_computation.1 | async-start | bytes 2097152 | tf_op jit(solution)/shard_map/all_to_all | solution.py:27
  71.1 15.9 %all-to-all-done.1 = bf16[16,128,256]{2,1,0:T(8,128)(2,1)} async-done(((bf16[16,128,256]{2,1,0:T(8,128)(2,1)}), bf16[16,128,256]{2,1,0:T(8,128)(2,1)}, u32[]{:S(2)}, u32[]{:S(2)}) %all-to-all-start.1) | async-done | bytes 1048608 | tf_op jit(solution)/shard_map/all_to_all | solution.py:27
  87.0 30.7 %all-gather.2.cloned.1.call-done = bf16[2048,768]{0,1:T(8,128)(2,1)} async-done(((bf16[256,768]{0,1:T(8,128)(2,1)}), bf16[2048,768]{0,1:T(8,128)(2,1)}) %all-gather.2.cloned.1.call-update) | async-done | bytes 3145744 | tf_op jit(solution)/shard_map/all_gather | solution.py:46
  117.7 77.5 %while.16 = (s32[]{:T(128)}, f32[2048,512]{0,1:T(8,128)}, f32[2048,2]{0,1:T(2,128)S(1)}, bf16[2048,2048]{1,0:T(8,128)(2,1)}, bf16[2048,768]{0,1:T(8,128)(2,1)}, ...) while((s32[]{:T(128)}, f32[2048,512]{0,1:T(8,128)}, ...), condition=%wide.region_4.0_spmd.clone, body=%wide.region_1.0_spmd.clone.sunk | while | flops 2162043904 | bytes 32319712 | solution.py:114
  117.7 1.2 constant_dynamic-slice_fusion.8
  119.3 0.2 fusion.52
  119.6 2.0 convolution_bitcast_fusion.5
  121.5 2.0 convolution_bitcast_fusion.4
  123.5 3.3 %fusion.51 = f32[2048,256]{0,1:T(8,128)S(1)} fusion(bf16[512,256]{0,1:T(8,128)(2,1)S(1)} %get-tuple-element.214, bf16[2048,256]{1,0:T(8,128)(2,1)} %get-tuple-element.247, bf16[2048,2048]{1,0:T(8,128)(2,1)} %get-tuple-element.245, s32[]{:T(128)S(6)} %select_n.10, bf16[2048,768]{0,1:T(8,128)(2,1)} %get-tuple-element.246), kind=kOutput, calls=%fused_computation.8.clone.1 | convolution fusion | flops 1076887552 | bytes 5768192 | tf_op jit(solution)/shard_map/while/body/eval_jaxpr/pq,pi->qi/dot_general | solution.py:104
  126.9 4.7 %fusion.50 = f32[2048,256]{0,1:T(8,128)} fusion(bf16[512,256]{0,1:T(8,128)(2,1)S(1)} %get-tuple-element.213, bf16[2048,256]{1,0:T(8,128)(2,1)} %get-tuple-element.247, bf16[2048,2048]{1,0:T(8,128)(2,1)} %get-tuple-element.245, s32[]{:T(128)S(6)} %select_n.10, bf16[2048,768]{0,1:T(8,128)(2,1)} %get-tuple-element.246), kind=kOutput, calls=%fused_computation.7.clone.1 | convolution fusion | flops 1076887552 | bytes 5768192 | tf_op jit(solution)/shard_map/while/body/eval_jaxpr/pq,pi->qi/dot_general | solution.py:104
  131.6 4.6 %maximum_add_fusion.4 = f32[2048,512]{0,1:T(8,128)} fusion(f32[2048,256]{0,1:T(8,128)} %fusion.50, f32[2048,256]{0,1:T(8,128)S(1)} %fusion.51, f32[2048,512]{0,1:T(8,128)} %get-tuple-element.231, pred[]{:T(512)S(6)} %compare.3), kind=kLoop, calls=%fused_computation.4.clone.1 | loop fusion | flops 3145728 | bytes 12582913 | tf_op jit(solution)/shard_map/while/body/eval_jaxpr/add | solution.py:112
  136.2 1.2 constant_dynamic-slice_fusion.8
  137.8 0.2 fusion.52
  138.0 2.0 convolution_bitcast_fusion.5
  140.0 2.0 convolution_bitcast_fusion.4
  142.0 3.3 %fusion.51 = f32[2048,256]{0,1:T(8,128)S(1)} fusion(bf16[512,256]{0,1:T(8,128)(2,1)S(1)} %get-tuple-element.214, bf16[2048,256]{1,0:T(8,128)(2,1)} %get-tuple-element.247, bf16[2048,2048]{1,0:T(8,128)(2,1)} %get-tuple-element.245, s32[]{:T(128)S(6)} %select_n.10, bf16[2048,768]{0,1:T(8,128)(2,1)} %get-tuple-element.246), kind=kOutput, calls=%fused_computation.8.clone.1 | convolution fusion | flops 1076887552 | bytes 5768192 | tf_op jit(solution)/shard_map/while/body/eval_jaxpr/pq,pi->qi/dot_general | solution.py:104
  145.3 4.7 %fusion.50 = f32[2048,256]{0,1:T(8,128)} fusion(bf16[512,256]{0,1:T(8,128)(2,1)S(1)} %get-tuple-element.213, bf16[2048,256]{1,0:T(8,128)(2,1)} %get-tuple-element.247, bf16[2048,2048]{1,0:T(8,128)(2,1)} %get-tuple-element.245, s32[]{:T(128)S(6)} %select_n.10, bf16[2048,768]{0,1:T(8,128)(2,1)} %get-tuple-element.246), kind=kOutput, calls=%fused_computation.7.clone.1 | convolution fusion | flops 1076887552 | bytes 5768192 | tf_op jit(solution)/shard_map/while/body/eval_jaxpr/pq,pi->qi/dot_general | solution.py:104
  150.0 5.8 %maximum_add_fusion.4 = f32[2048,512]{0,1:T(8,128)} fusion(f32[2048,256]{0,1:T(8,128)} %fusion.50, f32[2048,256]{0,1:T(8,128)S(1)} %fusion.51, f32[2048,512]{0,1:T(8,128)} %get-tuple-element.231, pred[]{:T(512)S(6)} %compare.3), kind=kLoop, calls=%fused_computation.4.clone.1 | loop fusion | flops 3145728 | bytes 12582913 | tf_op jit(solution)/shard_map/while/body/eval_jaxpr/add | solution.py:112
  155.9 1.2 constant_dynamic-slice_fusion.8
  157.7 2.0 convolution_bitcast_fusion.5
  159.7 2.0 convolution_bitcast_fusion.4
  161.7 3.3 %fusion.51 = f32[2048,256]{0,1:T(8,128)S(1)} fusion(bf16[512,256]{0,1:T(8,128)(2,1)S(1)} %get-tuple-element.214, bf16[2048,256]{1,0:T(8,128)(2,1)} %get-tuple-element.247, bf16[2048,2048]{1,0:T(8,128)(2,1)} %get-tuple-element.245, s32[]{:T(128)S(6)} %select_n.10, bf16[2048,768]{0,1:T(8,128)(2,1)} %get-tuple-element.246), kind=kOutput, calls=%fused_computation.8.clone.1 | convolution fusion | flops 1076887552 | bytes 5768192 | tf_op jit(solution)/shard_map/while/body/eval_jaxpr/pq,pi->qi/dot_general | solution.py:104
  165.0 4.7 %fusion.50 = f32[2048,256]{0,1:T(8,128)} fusion(bf16[512,256]{0,1:T(8,128)(2,1)S(1)} %get-tuple-element.213, bf16[2048,256]{1,0:T(8,128)(2,1)} %get-tuple-element.247, bf16[2048,2048]{1,0:T(8,128)(2,1)} %get-tuple-element.245, s32[]{:T(128)S(6)} %select_n.10, bf16[2048,768]{0,1:T(8,128)(2,1)} %get-tuple-element.246), kind=kOutput, calls=%fused_computation.7.clone.1 | convolution fusion | flops 1076887552 | bytes 5768192 | tf_op jit(solution)/shard_map/while/body/eval_jaxpr/pq,pi->qi/dot_general | solution.py:104
  169.7 5.8 %maximum_add_fusion.4 = f32[2048,512]{0,1:T(8,128)} fusion(f32[2048,256]{0,1:T(8,128)} %fusion.50, f32[2048,256]{0,1:T(8,128)S(1)} %fusion.51, f32[2048,512]{0,1:T(8,128)} %get-tuple-element.231, pred[]{:T(512)S(6)} %compare.3), kind=kLoop, calls=%fused_computation.4.clone.1 | loop fusion | flops 3145728 | bytes 12582913 | tf_op jit(solution)/shard_map/while/body/eval_jaxpr/add | solution.py:112
  175.5 1.2 constant_dynamic-slice_fusion.8
  177.4 2.0 convolution_bitcast_fusion.5
  179.3 2.0 convolution_bitcast_fusion.4
  181.4 3.3 %fusion.51 = f32[2048,256]{0,1:T(8,128)S(1)} fusion(bf16[512,256]{0,1:T(8,128)(2,1)S(1)} %get-tuple-element.214, bf16[2048,256]{1,0:T(8,128)(2,1)} %get-tuple-element.247, bf16[2048,2048]{1,0:T(8,128)(2,1)} %get-tuple-element.245, s32[]{:T(128)S(6)} %select_n.10, bf16[2048,768]{0,1:T(8,128)(2,1)} %get-tuple-element.246), kind=kOutput, calls=%fused_computation.8.clone.1 | convolution fusion | flops 1076887552 | bytes 5768192 | tf_op jit(solution)/shard_map/while/body/eval_jaxpr/pq,pi->qi/dot_general | solution.py:104
  184.7 4.7 %fusion.50 = f32[2048,256]{0,1:T(8,128)} fusion(bf16[512,256]{0,1:T(8,128)(2,1)S(1)} %get-tuple-element.213, bf16[2048,256]{1,0:T(8,128)(2,1)} %get-tuple-element.247, bf16[2048,2048]{1,0:T(8,128)(2,1)} %get-tuple-element.245, s32[]{:T(128)S(6)} %select_n.10, bf16[2048,768]{0,1:T(8,128)(2,1)} %get-tuple-element.246), kind=kOutput, calls=%fused_computation.7.clone.1 | convolution fusion | flops 1076887552 | bytes 5768192 | tf_op jit(solution)/shard_map/while/body/eval_jaxpr/pq,pi->qi/dot_general | solution.py:104
  189.4 5.8 %maximum_add_fusion.4 = f32[2048,512]{0,1:T(8,128)} fusion(f32[2048,256]{0,1:T(8,128)} %fusion.50, f32[2048,256]{0,1:T(8,128)S(1)} %fusion.51, f32[2048,512]{0,1:T(8,128)} %get-tuple-element.231, pred[]{:T(512)S(6)} %compare.3), kind=kLoop, calls=%fused_computation.4.clone.1 | loop fusion | flops 3145728 | bytes 12582913 | tf_op jit(solution)/shard_map/while/body/eval_jaxpr/add | solution.py:112
  195.2 2.5 convert_element_type.96
  197.7 0.3 pad_maximum_fusion
  198.0 2.6 copy.16
  200.6 67.9 %reduce-scatter.4.cloned.1.call-done = bf16[128,514]{1,0:T(8,128)(2,1)} async-done(((bf16[2048,514]{1,0:T(8,128)(2,1)}), bf16[128,514]{1,0:T(8,128)(2,1)}) %reduce-scatter.4.cloned.1.call-update) | async-done | bytes 131600
  268.5 0.8 split.8
  269.3 0.9 split.9
  270.8 32.8 %all_to_all.21 = bf16[16,128,512]{2,1,0:T(8,128)(2,1)S(1)} all-to-all(bf16[16,128,512]{2,1,0:T(8,128)(2,1)S(1)} %broadcast_in_dim.25), channel_id=1, replica_groups=mesh['row'=16,'col_0'=8,'col_1'=2] {'row'}, dimensions={0} | all-to-all | bytes 4194304 | tf_op jit(solution)/shard_map/all_to_all | solution.py:27
  303.6 0.5 convolution_convert_fusion.1
  304.1 0.5 convolution_convert_fusion.2
  304.6 19.0 %all_to_all.22 = bf16[16,16,2,128]{3,1,2,0:T(8,128)(2,1)S(1)} all-to-all(bf16[16,16,2,128]{3,1,2,0:T(8,128)(2,1)S(1)} %pad_maximum_fusion.3), channel_id=1, replica_groups=mesh['row'=16,'col_0'=8,'col_1'=2] {'col_0','col_1'}, dimensions={0} | all-to-all | bytes 262144 | tf_op jit(solution)/shard_map/all_to_all | solution.py:21
  323.7 0.6 copy.15
  (49 shorter events, 3.2 us)
Async XLA Ops:
  6.5 1.1 copy-start
  6.5 111.2 %all-gather.2.cloned.1.call-start = ((), (), s32[]{:S(2)}) async-start(), calls=%async_computation.5 | async-start | bytes 3538944 | tf_op jit(solution)/shard_map/all_gather | solution.py:46
  64.7 22.3 %all-to-all-start.1 = ((bf16[16,128,256]{2,1,0:T(8,128)(2,1)}), bf16[16,128,256]{2,1,0:T(8,128)(2,1)}, u32[]{:S(2)}, u32[]{:S(2)}) async-start(bf16[16,128,256]{2,1,0:T(8,128)(2,1)} %broadcast_in_dim.24), calls=%async_computation.1 | async-start | bytes 2097152 | tf_op jit(solution)/shard_map/all_to_all | solution.py:27
  71.1 197.4 %reduce-scatter.4.cloned.1.call-start = ((), (), s32[]{:S(2)}) async-start(), calls=%async_computation.6 | async-start | bytes 2785280
Sparse Core Ops, SparseCore 0:
  63.6 54.0 all-gather.1
  200.7 67.7 reduce-scatter.3
where the time goes:
time: 332 us; the launch traced here: 331 us
  waiting for transfers between devices  114 us (34%)
  blocking collectives  103 us (31%)
  matrix products  49.9 us (15%)
  other arithmetic  29.3 us (9%)
  local copies, waits for them, and re-layouts  13.8 us (4%)
  between operations  13.6 us (4%)
  starting transfers between devices  6.4 us (2%)
    unnamed x3, waiting for transfers between devices  67.9 us
    all_to_all x2, blocking collectives, summed_on_arrival(): lax.all_to_all(split_up(shard, dim, devices), axis, 0, 0, tiled=True)  63.3 us
    all_to_all x1, blocking collectives, copy_for_each(): lax.all_to_all(jnp.broadcast_to(shard[None], (devices, *shard.shape)), ax...  32.8 us
    dot_general x8, matrix products, advance(): jnp.einsum('pq,pi->qi', amplitude, x_rows, preferred_element_type=jnp.flo...  32.1 us
    all_gather x1, waiting for transfers between devices, gather_axes(): out = lax.all_gather(out, axes[number], axis=dim, tiled=True)  30.7 us
    add x4, other arithmetic, advance(): k_total + jnp.concatenate(k_parts, axis=1)  22 us
    all_to_all x1, waiting for transfers between devices, copy_for_each(): lax.all_to_all(jnp.broadcast_to(shard[None], (devices, *shard.shape)), ax...  15.9 us
    dot_general x8, matrix products, advance(): jnp.einsum('p,pq->q', density, v_rows, preferred_element_type=jnp.float32)  15.8 us
  transfers between devices with their start and end apart: 3, of which 3 were waited for; matrix products, arithmetic and copies ran while one was open for 0% of the time, Pallas kernels for 0%

commit v1 on v0

v1 whole, which is shorter than its diff:
```python
import jax
import jax.numpy as jnp
from jax import lax
from jax.experimental import pallas as pl
from jax.experimental.pallas import tpu as pltpu
from jax.sharding import Mesh
from jax.sharding import PartitionSpec as P

P_SIZE = 32768
ROW = ("yl", "x", "c")
CHIPS = ("yl", "x")
COL = ("z", "yh")
F32 = jnp.float32
BF16 = jnp.bfloat16
PAY = 784
LIMIT = pltpu.CompilerParams(vmem_limit_bytes=24 * 1024 * 1024)
VM = pl.BlockSpec(memory_space=pltpu.VMEM)
SM = pl.BlockSpec(memory_space=pltpu.SMEM)
HB = pl.BlockSpec(memory_space=pltpu.HBM)


def swap():
    return [(0, 1), (1, 0)]


def ring(size, step):
    return [(i, (i + step) % size) for i in range(size)]


def dot(a, b, dims):
    return lax.dot_general(a, b, (dims, ((), ())), preferred_element_type=F32)


def cost(flops, moved):
    return pl.CostEstimate(flops=flops, transcendentals=0, bytes_accessed=moved)


def encode_kernel(mine, got, trial, greens, other, out):
    def step(j, _):
        rows = jnp.concatenate([mine[j], got[j]], axis=1)
        x_side = jnp.concatenate([trial[...], other[0:256]], axis=1)
        out[j, 0:256] = dot(x_side, rows, ((1,), (1,))).astype(BF16)
        for w in range(2):
            side = jnp.concatenate([greens[w], other[256 * (w + 1):256 * (w + 2)]], axis=1)
            theta = dot(rows, side, ((1,), (1,))).astype(BF16)
            for h in range(2):
                at = 256 * (w + 1) + 128 * h
                out[j, at:at + 128] = theta[:, 128 * h:128 * (h + 1)]
        return 0

    lax.fori_loop(0, 8, step, 0, unroll=2)


def encode(*args):
    return pl.pallas_call(
        encode_kernel,
        in_specs=[VM] * 5,
        out_specs=VM,
        out_shape=jax.ShapeDtypeStruct((8, 768, 128), BF16),
        compiler_params=LIMIT,
        cost_estimate=cost(2 * 1024 * 256 * 768, 3 << 20),
        name="encode",
    )(*args)


def own_kernel(parts, out, spread):
    total = parts[0].astype(F32)
    for j in range(1, 8):
        total = total + parts[j].astype(F32)
    total = total.astype(BF16)
    out[0:768] = total
    for j in range(8):
        spread[j] = total[0:256]
    wide = total.astype(F32)
    rows = []
    for w in range(2):
        at = 256 * (w + 1)
        acc = jnp.sum(wide[0:128] * wide[at:at + 128].T, axis=0, keepdims=True)
        acc = acc + jnp.sum(wide[128:256] * wide[at + 128:at + 256].T, axis=0, keepdims=True)
        rows.append(acc)
    rows.append(jnp.zeros((14, 128), F32))
    out[768:784] = jnp.concatenate(rows, axis=0).astype(BF16)


def own_points(parts):
    return pl.pallas_call(
        own_kernel,
        in_specs=[VM],
        out_specs=[VM, VM],
        out_shape=[jax.ShapeDtypeStruct((PAY, 128), BF16), jax.ShapeDtypeStruct((8, 256, 128), BF16)],
        compiler_params=LIMIT,
        cost_estimate=cost(1 << 24, 2 << 20),
        name="own",
    )(parts)


def make_exchange_kernel(blocks, where, first, last):
    def kernel(pos, *refs):
        pays = refs[:blocks]
        kern, same, cross = refs[blocks:blocks + 3]
        rest = refs[blocks + 3:]
        v_buf, sems = rest[-2:]
        rest = rest[:-2]
        if not first:
            e_in, u_in = rest[:2]
            rest = rest[2:]
        core = pos[0]
        copies = []
        for h in range(2):
            for b in range(blocks):
                lanes = pl.ds(1024 * h, 1024)
                copies.append(
                    pltpu.make_async_copy(
                        kern.at[pos[1 + where[b]], :, lanes],
                        v_buf.at[h, pl.ds(128 * b, 128)],
                        sems.at[h, b],
                    )
                )
        for cp in copies:
            cp.start()
        xp = jnp.concatenate([p[0:256] for p in pays], axis=1)
        dens = jnp.concatenate([p[768:784] for p in pays], axis=1)

        def theta(w):
            at = 256 * (w + 1)
            return jnp.concatenate(
                [jnp.concatenate([p[at:at + 128], p[at + 128:at + 256]], axis=1) for p in pays], axis=0
            )

        flag = core == 0
        for h in range(2):
            for b in range(blocks):
                copies[h * blocks + b].wait()

            def chip_step(i, _):
                chip = 4 * h + i
                lanes = pl.ds(pl.multiple_of(256 * chip, 256), 256)
                a = same[chip]
                b = cross[chip]
                xq = jnp.concatenate([jnp.where(flag, a, b), jnp.where(flag, b, a)], axis=1)
                v = v_buf[h, :, pl.ds(pl.multiple_of(256 * i, 256), 256)]
                u = dot(dens, v, ((1,), (0,)))
                if not first:
                    u = u + u_in[:, lanes]
                if not last:
                    rest[1][:, lanes] = u
                wide = v.astype(F32)
                for w in range(2):
                    tile = dot(theta(w), xq, ((1,), (0,)))
                    amp = (wide * tile).astype(BF16)
                    e = dot(xp, amp, ((1,), (0,)))
                    rows = slice(256 * w, 256 * (w + 1))
                    if not first:
                        e = e + e_in[rows, lanes]
                    if not last:
                        rest[0][rows, lanes] = e
                    else:
                        f = (u[w:w + 1] * xq.astype(F32) - e).astype(BF16)
                        here = pl.ds(pl.multiple_of(128 * chip, 128), 128)
                        low, high = f[:, 0:128], f[:, 128:256]
                        rest[0][rows, here] = jnp.where(flag, low, high)
                        rest[1][rows, here] = jnp.where(flag, high, low)
                return 0

            lax.fori_loop(0, 4, chip_step, 0)

    return kernel


def exchange(pos, pays, where, coulomb, same, cross, totals, last):
    blocks = len(pays)
    first = totals is None
    args = [pos, *pays, coulomb, same, cross]
    in_specs = [SM] + [VM] * blocks + [HB, VM, VM]
    alias = {}
    if not first:
        if not last:
            alias = {len(args): 0, len(args) + 1: 1}
        args += list(totals)
        in_specs += [VM, VM]
    if last:
        out_shape = [jax.ShapeDtypeStruct((512, 1024), BF16)] * 2
    else:
        out_shape = [jax.ShapeDtypeStruct((512, 2048), F32), jax.ShapeDtypeStruct((16, 2048), F32)]
    rows = 128 * blocks
    return pl.pallas_call(
        make_exchange_kernel(blocks, where, first, last),
        in_specs=in_specs,
        out_specs=[VM, VM],
        out_shape=out_shape,
        scratch_shapes=[pltpu.VMEM((2, rows, 1024), BF16), pltpu.SemaphoreType.DMA((2, blocks))],
        input_output_aliases=alias,
        compiler_params=LIMIT,
        cost_estimate=cost(8 * rows * 2048 * 256, 8 << 20),
        name="exchange",
    )(*args)


def decode_kernel(pos, f_mine, f_got, *refs):
    cols = refs[:8]
    keep, give = refs[8:]
    f = (f_mine[...].astype(F32) + f_got[...].astype(F32)).astype(BF16)
    for j in range(8):
        chip = lax.bitwise_xor(pos[17], j // 4) * 4 + lax.rem(pos[18] - j % 4 + 4, 4)
        g = dot(f, jnp.concatenate([cols[j][0], cols[j][1]], axis=1), ((1,), (0,)))
        keep[chip] = g[:, 0:128].astype(BF16)
        give[chip] = g[:, 128:256].astype(BF16)


def decode(pos, f, f_got, cols):
    return pl.pallas_call(
        decode_kernel,
        in_specs=[SM] + [VM] * 10,
        out_specs=[VM, VM],
        out_shape=[jax.ShapeDtypeStruct((8, 512, 128), BF16)] * 2,
        compiler_params=LIMIT,
        cost_estimate=cost(2 * 512 * 1024 * 2048, 8 << 20),
        name="decode",
    )(pos, f, f_got, *cols)


def sum_kernel(parts, out):
    total = parts[0].astype(F32)
    for j in range(1, 8):
        total = total + parts[j].astype(F32)
    total = total.astype(BF16)
    for w in range(2):
        for c in range(16):
            out[c, w] = total[256 * w + 16 * c:256 * w + 16 * (c + 1)]


def x_shift(a, step):
    return lax.ppermute(a, "x", ring(4, step))


def on_device(collocation, greens, trial_orbitals, coulomb):
    yl, x, c = lax.axis_index("yl"), lax.axis_index("x"), lax.axis_index("c")
    z, yh = lax.axis_index("z"), lax.axis_index("yh")
    near = [(0, 0)] + [(s, 0) for s in (1, 2, 3, 4)] + [(-s, 0) for s in (1, 2, 3)]
    near += [(0, 1)] + [(s, 1) for s in (1, 2, 3)] + [(-s, 1) for s in (1, 2, 3, 4)]
    index = {key: n for n, key in enumerate(near)}
    places = [lax.rem(z - s + 8, 8) * 2 + (yh if flip == 0 else 1 - yh) for s, flip in near]
    pos = jnp.stack([c, *places, yl, x]).astype(jnp.int32)

    halves = collocation.reshape(8, 2, 128, 128)
    mine = lax.dynamic_index_in_dim(halves, c, 1, keepdims=False)
    give = lax.dynamic_index_in_dim(halves, 1 - c, 1, keepdims=False)
    stacked = jnp.concatenate([trial_orbitals, greens.reshape(512, 128)], axis=0)
    got = lax.ppermute(give, "c", swap())
    other = lax.ppermute(stacked, "c", swap())
    partial_value = encode(mine, got, trial_orbitals, greens, other)
    parts = lax.all_to_all(partial_value, CHIPS, 0, 0, tiled=True)
    own, spread = own_points(parts)

    pay = {(0, 0): own}
    pay[(0, 1)] = lax.ppermute(own, "yh", swap())

    def hop(s):
        for flip in (0, 1):
            for sign in (1, -1):
                if (sign * s, flip) in index:
                    pay[(sign * s, flip)] = lax.ppermute(
                        pay[(sign * (s - 1), flip)], "z", ring(8, sign)
                    )

    hop(1)
    same = lax.all_to_all(spread, CHIPS, 0, 0, tiled=True)
    cross = lax.ppermute(same, "c", swap())

    def held(keys, others):
        got = lax.optimization_barrier(tuple(pay[k] for k in keys) + tuple(others))
        for k, v in zip(keys, got):
            pay[k] = v
        return got[len(keys):]

    def stage(s):
        return [k for k in near if abs(k[0]) == s]

    def add(stages, totals, last=False):
        keys = [k for k in near if abs(k[0]) in stages]
        return exchange(pos, [pay[k] for k in keys], [index[k] for k in keys], coulomb, same, cross, totals, last)

    base = jnp.stack([mine.reshape(1024, 128), got.reshape(1024, 128)])
    base, same = lax.optimization_barrier((base, same))
    cols = [base] + [None] * 7
    cols[4] = lax.ppermute(base, "yl", swap())
    cols[1] = x_shift(base, 1)
    cols[3] = x_shift(base, -1)
    hop(2)
    totals = add((0, 1), None)
    cols[4], cols[1], cols[3] = held(stage(2), (cols[4], cols[1], cols[3]))
    cols[5] = x_shift(cols[4], 1)
    cols[7] = x_shift(cols[4], -1)
    cols[2] = x_shift(cols[1], 1)
    hop(3)
    totals = add((2,), totals)
    cols[2], cols[5], cols[7] = held(stage(3), (cols[2], cols[5], cols[7]))
    cols[6] = lax.ppermute(cols[2], "yl", swap())
    hop(4)
    totals = add((3,), totals)
    f_mine, f_give = add((4,), totals, True)
    f_got = lax.ppermute(f_give, "c", swap())
    keep, send = decode(pos, f_mine, f_got, cols)
    back = lax.ppermute(send, "c", swap())
    both = (keep.astype(F32) + back.astype(F32)).astype(BF16)
    terms = lax.all_to_all(both, CHIPS, 0, 0, tiled=True)
    summed = pl.pallas_call(
        sum_kernel,
        in_specs=[VM],
        out_specs=VM,
        out_shape=jax.ShapeDtypeStruct((16, 2, 16, 128), BF16),
        compiler_params=LIMIT,
        name="chip_sum",
    )(terms)
    shares = lax.all_to_all(summed, COL, 0, 0, tiled=True)
    total = jnp.sum(shares.astype(F32), axis=0) * P_SIZE ** (-0.5)
    return jnp.swapaxes(total, 0, 1).astype(BF16)


def solution(mesh):
    finer = Mesh(mesh.devices.reshape(2, 4, 2, 8, 2), ("yl", "x", "c", "z", "yh"))
    placed = (P(COL, ROW), P(None, None, ROW), P(None, ROW), P(None, ROW, COL))
    return jax.shard_map(
        on_device, mesh=finer, in_specs=placed, out_specs=P(COL, None, ROW), check_vma=False
    )
```

time: 332 us -> 187 us (0.56)
  waiting for transfers between devices: 114 us -> 34.8 us
  matrix products: 49.9 us -> 0 us
  blocking collectives: 103 us -> 59.7 us
  starting transfers between devices: 6.4 us -> 49.5 us
  Pallas kernels: 0 us -> 30.4 us
  other arithmetic: 29.3 us -> 1.28 us
  between operations: 13.6 us -> 0.26 us
    unnamed x3 -> x0, waiting for transfers between devices: 67.9 us -> none
    dot_general x19 -> x0, matrix products: 49.9 us -> none  [the longest x8 32.1 us: advance(): jnp.einsum('pq,pi->qi', amplitude, x_rows, preferred_element_type=jnp.flo...]
    ppermute x0 -> x27, starting transfers between devices: none -> 46 us  [the longest x14 24.8 us: hop(): lax.ppermute(pay[sign * (s - 1), flip], 'z', ring(8, sign))]
    all_to_all x3, blocking collectives: 96.1 us -> 59.7 us  [the longest x1 24.6 us: on_device(): parts = lax.all_to_all(partial_value, CHIPS, 0, 0, tiled=True)]
    ppermute x0 -> x27, waiting for transfers between devices: none -> 34.8 us  [the longest x14 13.7 us: hop(): lax.ppermute(pay[sign * (s - 1), flip], 'z', ring(8, sign))]
    all_gather x1 -> x0, waiting for transfers between devices: 30.7 us -> none  [gather_axes(): out = lax.all_gather(out, axes[number], axis=dim, tiled=True)]
    pallas_call x0 -> x8, Pallas kernels: none -> 30.4 us  [the longest x4 24.1 us: exchange(): pl.pallas_call(make_exchange_kernel(blocks, where, first, last), in_specs...]
    add x8 -> x0, other arithmetic: 22.2 us -> none  [the longest x4 22 us: advance(): k_total + jnp.concatenate(k_parts, axis=1)]
  transfers between devices with their start and end apart: 3 -> 28, of which waited for: 3 -> 8; matrix products, arithmetic and copies ran while one was open for 0% -> 1% of each run, Pallas kernels for 0% -> 11%
where the time goes in v1:
time: 187 us; the launch traced here: 186 us
  blocking collectives  59.7 us (32%)
  starting transfers between devices  49.5 us (26%)
  waiting for transfers between devices  34.8 us (19%)
  Pallas kernels  30.4 us (16%)
  local copies, waits for them, and re-layouts  10.5 us (6%)
    ppermute x14, starting transfers between devices, hop(): lax.ppermute(pay[sign * (s - 1), flip], 'z', ring(8, sign))  24.8 us
    all_to_all x1, blocking collectives, on_device(): parts = lax.all_to_all(partial_value, CHIPS, 0, 0, tiled=True)  24.6 us
    pallas_call x4, Pallas kernels, exchange(): pl.pallas_call(make_exchange_kernel(blocks, where, first, last), in_specs...  24.1 us
    all_to_all x1, blocking collectives, on_device(): terms = lax.all_to_all(both, CHIPS, 0, 0, tiled=True)  18.7 us
    all_to_all x1, blocking collectives, on_device(): shares = lax.all_to_all(summed, COL, 0, 0, tiled=True)  16.4 us
    ppermute x14, waiting for transfers between devices, hop(): lax.ppermute(pay[sign * (s - 1), flip], 'z', ring(8, sign))  13.7 us
    ppermute x1, waiting for transfers between devices, on_device(): cols[6] = lax.ppermute(cols[2], 'yl', swap())  12.6 us
    unnamed x24, local copies, waits for them, and re-layouts  8.75 us
  transfers between devices with their start and end apart: 28, of which 8 were waited for; matrix products, arithmetic and copies ran while one was open for 1% of the time, Pallas kernels for 11%

profile of v1, /device:TPU:1, one launch (start us, length us, event | category | flops | bytes accessed | tf_op | source)
XLA Modules:
  0.0 186.4 jit_solution(13896918036497817872)
XLA Ops:
  0.0 1.1 dynamic-slice_bitcast_fusion
  1.1 3.3 %collective-permute-start = (bf16[8,128,128]{2,1,0:T(8,128)(2,1)S(1)}, bf16[8,128,128]{2,1,0:T(8,128)(2,1)S(1)}, u32[]{:S(2)}, u32[]{:S(2)}) collective-permute-start(bf16[8,128,128]{2,1,0:T(8,128)(2,1)S(1)} %get-tuple-element.61), channel_id=1, source_target_pairs={{0,16},{16,0},{1,17},{17,1},{2,18},{18,2},{3,19},{19,3},{4,20},{20... | collective-permute-start | bytes 786440 | tf_op jit(solution)/shard_map/ppermute | solution.py:249
  4.4 0.9 pad_maximum_fusion.1
  5.4 1.4 collective-permute-done.1.other
  6.8 0.9 copy-done.2
  7.7 0.8 copy-done.3
  8.6 1.3 encode.1
  9.9 24.6 %all_to_all.20.parts = bf16[8,768,128]{2,1,0:T(8,128)(2,1)S(1)} all-to-all(bf16[8,768,128]{2,1,0:T(8,128)(2,1)S(1)} %encode.1), channel_id=1, replica_groups=mesh['yl'=2,'x'=4,'c'=2,'z'=8,'yh'=2] {'yl','x'}, dimensions={0} | all-to-all | bytes 3145728 | tf_op jit(solution)/shard_map/all_to_all | solution.py:252
  34.5 1.0 own.1
  35.5 3.5 %all-to-all-start.1 = ((bf16[8,256,128]{2,1,0:T(8,128)(2,1)}), bf16[8,256,128]{2,1,0:T(8,128)(2,1)S(1)}, u32[]{:S(2)}, u32[]{:S(2)}) async-start(bf16[8,256,128]{2,1,0:T(8,128)(2,1)} %get-tuple-element.34), calls=%async_computation.1 | async-start | bytes 1048576 | tf_op jit(solution)/shard_map/all_to_all | solution.py:267
  39.0 2.7 %collective-permute-start.6 = (bf16[784,128]{1,0:T(8,128)(2,1)S(1)}, bf16[784,128]{1,0:T(8,128)(2,1)S(1)}, u32[]{:S(2)}, u32[]{:S(2)}) collective-permute-start(bf16[784,128]{1,0:T(8,128)(2,1)S(1)} %get-tuple-element.33.refs_0_), channel_id=1, source_target_pairs={{0,1},{1,0},{2,3},{3,2},{4,5},{5,4},{6,7},{7,6},{8,9},{9,8},{10,11... | collective-permute-start | bytes 602120 | tf_op jit(solution)/shard_map/ppermute | solution.py:256
  41.7 1.6 collective-permute-start.2
  43.4 3.9 %collective-permute-start.4 = (bf16[784,128]{1,0:T(8,128)(2,1)S(1)}, bf16[784,128]{1,0:T(8,128)(2,1)}, u32[]{:S(2)}, u32[]{:S(2)}) collective-permute-start(bf16[784,128]{1,0:T(8,128)(2,1)S(1)} %get-tuple-element.33.refs_0_), channel_id=1, source_target_pairs={{0,14},{2,0},{4,2},{6,4},{8,6},{10,8},{12,10},{14,12},{1,15},{3,1}... | collective-permute-start | bytes 602120 | tf_op jit(solution)/shard_map/ppermute | solution.py:262
  47.3 4.7 %collective-permute-done.6.refs_3_ = bf16[784,128]{1,0:T(8,128)(2,1)S(1)} collective-permute-done((bf16[784,128]{1,0:T(8,128)(2,1)S(1)}, bf16[784,128]{1,0:T(8,128)(2,1)S(1)}, u32[]{:S(2)}, u32[]{:S(2)}) %collective-permute-start.6) | collective-permute-done | bytes 200736 | tf_op jit(solution)/shard_map/ppermute | solution.py:256
  52.0 1.6 collective-permute-start.7
  53.7 3.9 %collective-permute-start.9 = (bf16[784,128]{1,0:T(8,128)(2,1)S(1)}, bf16[784,128]{1,0:T(8,128)(2,1)}, u32[]{:S(2)}, u32[]{:S(2)}) collective-permute-start(bf16[784,128]{1,0:T(8,128)(2,1)S(1)} %collective-permute-done.6.refs_3_), channel_id=1, source_target_pairs={{0,14},{2,0},{4,2},{6,4},{8,6},{10,8},{12,10},{14,12},{1,15},{3,1}... | collective-permute-start | bytes 602120 | tf_op jit(solution)/shard_map/ppermute | solution.py:262
  57.6 2.7 %collective-permute-start.5 = (bf16[784,128]{1,0:T(8,128)(2,1)}, bf16[784,128]{1,0:T(8,128)(2,1)S(1)}, u32[]{:S(2)}, u32[]{:S(2)}) collective-permute-start(bf16[784,128]{1,0:T(8,128)(2,1)} %collective-permute-done.4.refs_2_), channel_id=1, source_target_pairs={{0,14},{2,0},{4,2},{6,4},{8,6},{10,8},{12,10},{14,12},{1,15},{3,1}... | collective-permute-start | bytes 602120 | tf_op jit(solution)/shard_map/ppermute | solution.py:262
  60.4 0.7 collective-permute-start.11
  61.0 0.7 collective-permute-done.7.refs_4_
  61.7 0.8 collective-permute-start.12
  62.5 2.4 %collective-permute-start.13 = (bf16[2,1024,128]{2,1,0:T(8,128)(2,1)S(1)}, bf16[2,1024,128]{2,1,0:T(8,128)(2,1)S(1)}, u32[]{:S(2)}, u32[]{:S(2)}) collective-permute-start(bf16[2,1024,128]{2,1,0:T(8,128)(2,1)S(1)} %pad_maximum_fusion.refs_0_), channel_id=1, source_target_pairs={{0,96},{32,0},{64,32},{96,64},{1,97},{33,1},{65,33},{97,65},{2,98}... | collective-permute-start | bytes 1572872 | tf_op jit(solution)/shard_map/ppermute | solution.py:233
  64.9 1.0 collective-permute-done.3.refs_0_
  65.9 2.6 %collective-permute-start.23 = (bf16[8,256,128]{2,1,0:T(8,128)(2,1)S(1)}, bf16[8,256,128]{2,1,0:T(8,128)(2,1)S(1)}, u32[]{:S(2)}, u32[]{:S(2)}) collective-permute-start(bf16[8,256,128]{2,1,0:T(8,128)(2,1)S(1)} %all-to-all-done.1.refs_7_.refs_5_.refs_3_), channel_id=1, source_target_pairs={{0,16},{16,0},{1,17},{17,1},{2,18},{18,2},{3,19},{19,3},{4,20},{20... | collective-permute-start | bytes 1572872 | tf_op jit(solution)/shard_map/ppermute | solution.py:268
  68.5 2.3 %collective-permute-start.10 = (bf16[784,128]{1,0:T(8,128)(2,1)}, bf16[784,128]{1,0:T(8,128)(2,1)S(1)}, u32[]{:S(2)}, u32[]{:S(2)}) collective-permute-start(bf16[784,128]{1,0:T(8,128)(2,1)} %collective-permute-done.9.refs_5_), channel_id=1, source_target_pairs={{0,14},{2,0},{4,2},{6,4},{8,6},{10,8},{12,10},{14,12},{1,15},{3,1}... | collective-permute-start | bytes 602120 | tf_op jit(solution)/shard_map/ppermute | solution.py:262
  70.8 4.6 %collective-permute-done.10.refs_3_ = bf16[784,128]{1,0:T(8,128)(2,1)S(1)} collective-permute-done((bf16[784,128]{1,0:T(8,128)(2,1)}, bf16[784,128]{1,0:T(8,128)(2,1)S(1)}, u32[]{:S(2)}, u32[]{:S(2)}) %collective-permute-start.10) | collective-permute-done | bytes 200736 | tf_op jit(solution)/shard_map/ppermute | solution.py:262
  75.8 7.5 %collective-permute-done.8.refs_2_ = bf16[784,128]{1,0:T(8,128)(2,1)S(1)} collective-permute-done((bf16[784,128]{1,0:T(8,128)(2,1)}, bf16[784,128]{1,0:T(8,128)(2,1)S(1)}, u32[]{:S(2)}, u32[]{:S(2)}) %collective-permute-start.8) | collective-permute-done | bytes 200736 | tf_op jit(solution)/shard_map/ppermute | solution.py:262
  83.3 0.8 copy-done.4
  84.2 1.1 collective-permute-start.19
  85.2 1.6 collective-permute-start.20
  87.1 2.7 %collective-permute-start.15 = (bf16[784,128]{1,0:T(8,128)(2,1)S(1)}, bf16[784,128]{1,0:T(8,128)(2,1)S(1)}, u32[]{:S(2)}, u32[]{:S(2)}) collective-permute-start(bf16[784,128]{1,0:T(8,128)(2,1)S(1)} %collective-permute-done.5.refs_1_), channel_id=1, source_target_pairs={{0,14},{2,0},{4,2},{6,4},{8,6},{10,8},{12,10},{14,12},{1,15},{3,1}... | collective-permute-start | bytes 602120 | tf_op jit(solution)/shard_map/ppermute | solution.py:262
  89.7 3.4 %copy-done = bf16[16,128,2048]{2,1,0:T(8,128)(2,1)S(1)} copy-done((bf16[16,128,2048]{2,1,0:T(8,128)(2,1)S(1)}, bf16[16,128,2048]{2,1,0:T(8,128)(2,1)}, u32[]{:S(2)}) %copy-start) | copy-done | bytes 8388632
  93.1 0.9 copy-done.7
  94.0 0.9 copy-done.9
  95.0 0.9 copy-done.11
  95.9 7.6 %exchange.4 = (f32[512,2048]{1,0:T(8,128)S(1)}, f32[16,2048]{1,0:T(8,128)S(1)}) custom-call(s32[19]{0:T(128)S(1)} %stack.82.pos, bf16[784,128]{1,0:T(8,128)(2,1)S(1)} %copy-done.7, bf16[784,128]{1,0:T(8,128)(2,1)S(1)} %copy-done.11, bf16[784,128]{1,0:T(8,128)(2,1)} %collective-permute-done.4.refs_2_, bf16[784,128]{1,0:T(8,128)(2,1)S(1)} %copy-done.9, ...), custom_call_target="tpu_custom_call" | custom-call | flops 3221225472 | bytes 8388608 | tf_op jit(solution)/shard_map/exchange/pallas_call | solution.py:186
  103.6 2.7 %collective-permute-start.17 = (bf16[784,128]{1,0:T(8,128)(2,1)S(1)}, bf16[784,128]{1,0:T(8,128)(2,1)S(1)}, u32[]{:S(2)}, u32[]{:S(2)}) collective-permute-start(bf16[784,128]{1,0:T(8,128)(2,1)S(1)} %collective-permute-done.10.refs_3_), channel_id=1, source_target_pairs={{0,14},{2,0},{4,2},{6,4},{8,6},{10,8},{12,10},{14,12},{1,15},{3,1}... | collective-permute-start | bytes 602120 | tf_op jit(solution)/shard_map/ppermute | solution.py:262
  106.3 6.0 %exchange.5 = (f32[512,2048]{1,0:T(8,128)S(1)}, f32[16,2048]{1,0:T(8,128)S(1)}) custom-call(s32[19]{0:T(128)S(1)} %stack.82.pos, bf16[784,128]{1,0:T(8,128)(2,1)S(1)} %collective-permute-done.3.refs_0_, bf16[784,128]{1,0:T(8,128)(2,1)S(1)} %collective-permute-done.5.refs_1_, ...), custom_call_target="tpu_custom_call", output_to_operand_aliasing={{0}: (8, {}), {1}: (9, {})} | custom-call | flops 2147483648 | bytes 8388608 | tf_op jit(solution)/shard_map/exchange/pallas_call | solution.py:186
  112.5 2.7 %collective-permute-start.22 = (bf16[784,128]{1,0:T(8,128)(2,1)S(1)}, bf16[784,128]{1,0:T(8,128)(2,1)S(1)}, u32[]{:S(2)}, u32[]{:S(2)}) collective-permute-start(bf16[784,128]{1,0:T(8,128)(2,1)S(1)} %collective-permute-done.17.refs_3_), channel_id=1, source_target_pairs={{0,14},{2,0},{4,2},{6,4},{8,6},{10,8},{12,10},{14,12},{1,15},{3,1}... | collective-permute-start | bytes 602120 | tf_op jit(solution)/shard_map/ppermute | solution.py:262
  115.1 6.0 %exchange.6 = (f32[512,2048]{1,0:T(8,128)S(1)}, f32[16,2048]{1,0:T(8,128)S(1)}) custom-call(s32[19]{0:T(128)S(1)} %stack.82.pos, bf16[784,128]{1,0:T(8,128)(2,1)S(1)} %collective-permute-done.14.refs_0_, bf16[784,128]{1,0:T(8,128)(2,1)S(1)} %collective-permute-done.15.refs_1_, ...), custom_call_target="tpu_custom_call", output_to_operand_aliasing={{0}: (8, {}), {1}: (9, {})} | custom-call | flops 2147483648 | bytes 8388608 | tf_op jit(solution)/shard_map/exchange/pallas_call | solution.py:186
  121.2 4.5 %exchange.7 = (bf16[512,1024]{1,0:T(8,128)(2,1)S(1)}, bf16[512,1024]{1,0:T(8,128)(2,1)S(1)}) custom-call(s32[19]{0:T(128)S(1)} %stack.82.pos, bf16[784,128]{1,0:T(8,128)(2,1)S(1)} %collective-permute-done.21.refs_0_, bf16[784,128]{1,0:T(8,128)(2,1)S(1)} %collective-permute-done.22.refs_1_, bf16[16,128,2048]{2,1,0:T(8,128)(2,1)S(1)} %copy-done.1, ...), custom_call_target="tpu_custom_call" | custom-call | flops 1073741824 | bytes 8388608 | tf_op jit(solution)/shard_map/exchange/pallas_call | solution.py:186
  125.7 3.8 %collective-permute-start.24 = (bf16[512,1024]{1,0:T(8,128)(2,1)S(1)}, bf16[512,1024]{1,0:T(8,128)(2,1)S(1)}, u32[]{:S(2)}, u32[]{:S(2)}) collective-permute-start(bf16[512,1024]{1,0:T(8,128)(2,1)S(1)} %get-tuple-element.54), channel_id=1, source_target_pairs={{0,16},{16,0},{1,17},{17,1},{2,18},{18,2},{3,19},{19,3},{4,20},{20... | collective-permute-start | bytes 3145736 | tf_op jit(solution)/shard_map/ppermute | solution.py:302
  129.5 0.8 collective-permute-start.25
  130.3 12.6 %collective-permute-done.25.refs_6_ = bf16[2,1024,128]{2,1,0:T(8,128)(2,1)S(1)} collective-permute-done((bf16[2,1024,128]{2,1,0:T(8,128)(2,1)}, bf16[2,1024,128]{2,1,0:T(8,128)(2,1)S(1)}, u32[]{:S(2)}, u32[]{:S(2)}) %collective-permute-start.25) | collective-permute-done | bytes 524320 | tf_op jit(solution)/shard_map/ppermute | solution.py:298
  142.9 3.8 %decode.1 = (bf16[8,512,128]{2,1,0:T(8,128)(2,1)S(1)}, bf16[8,512,128]{2,1,0:T(8,128)(2,1)S(1)}) custom-call(s32[19]{0:T(128)S(1)} %stack.82.pos, bf16[512,1024]{1,0:T(8,128)(2,1)S(1)} %get-tuple-element.53.f_mine, bf16[512,1024]{1,0:T(8,128)(2,1)S(1)} %collective-permute-done.24.f_got, bf16[2,1024,128]{2,1,0:T(8,128)(2,1)S(1)} %pad_maximum_fusion.refs_0_, ...), custom_call_target="tpu_custom_call" | custom-call | flops 2147483648 | bytes 8388608 | tf_op jit(solution)/shard_map/decode/pallas_call | solution.py:211
  146.7 1.3 collective-permute-start.26
  148.0 2.3 %collective-permute-done.26 = bf16[8,512,128]{2,1,0:T(8,128)(2,1)S(1)} collective-permute-done((bf16[8,512,128]{2,1,0:T(8,128)(2,1)S(1)}, bf16[8,512,128]{2,1,0:T(8,128)(2,1)S(1)}, u32[]{:S(2)}, u32[]{:S(2)}) %collective-permute-start.26) | collective-permute-done | bytes 1048608 | tf_op jit(solution)/shard_map/ppermute | solution.py:304
  150.5 18.7 %all_to_all.21.parts = bf16[8,512,128]{2,1,0:T(8,128)(2,1)S(1)} all-to-all(bf16[8,512,128]{2,1,0:T(8,128)(2,1)S(1)} %add_convert_fusion), channel_id=1, replica_groups=mesh['yl'=2,'x'=4,'c'=2,'z'=8,'yh'=2] {'yl','x'}, dimensions={0} | all-to-all | bytes 2097152 | tf_op jit(solution)/shard_map/all_to_all | solution.py:306
  169.4 16.4 %all_to_all.22 = bf16[16,2,16,128]{3,2,1,0:T(8,128)(2,1)S(1)} all-to-all(bf16[16,2,16,128]{3,2,1,0:T(8,128)(2,1)S(1)} %chip_sum.1), channel_id=1, replica_groups=mesh['yl'=2,'x'=4,'c'=2,'z'=8,'yh'=2] {'z','yh'}, dimensions={0} | all-to-all | bytes 262144 | tf_op jit(solution)/shard_map/all_to_all | solution.py:315
  (51 shorter events, 2.0 us)
Async XLA Ops:
  1.1 5.7 %collective-permute-start = (bf16[8,128,128]{2,1,0:T(8,128)(2,1)S(1)}, bf16[8,128,128]{2,1,0:T(8,128)(2,1)S(1)}, u32[]{:S(2)}, u32[]{:S(2)}) collective-permute-start(bf16[8,128,128]{2,1,0:T(8,128)(2,1)S(1)} %get-tuple-element.61), channel_id=1, source_target_pairs={{0,16},{16,0},{1,17},{17,1},{2,18},{18,2},{3,19},{19,3},{4,20},{20... | collective-permute-start | bytes 786440 | tf_op jit(solution)/shard_map/ppermute | solution.py:249
  5.3 1.5 collective-permute-start.1
  6.8 0.9 copy-start.2
  7.7 0.8 copy-start.3
  35.5 24.8 %copy-start.6 = (bf16[784,128]{1,0:T(8,128)(2,1)}, bf16[784,128]{1,0:T(8,128)(2,1)S(1)}, u32[]{:S(2)}) copy-start(bf16[784,128]{1,0:T(8,128)(2,1)S(1)} %get-tuple-element.33.refs_0_) | copy-start | bytes 602116
  35.5 24.8 %all-to-all-start.1 = ((bf16[8,256,128]{2,1,0:T(8,128)(2,1)}), bf16[8,256,128]{2,1,0:T(8,128)(2,1)S(1)}, u32[]{:S(2)}, u32[]{:S(2)}) async-start(bf16[8,256,128]{2,1,0:T(8,128)(2,1)} %get-tuple-element.34), calls=%async_computation.1 | async-start | bytes 1048576 | tf_op jit(solution)/shard_map/all_to_all | solution.py:267
  39.0 13.0 %collective-permute-start.6 = (bf16[784,128]{1,0:T(8,128)(2,1)S(1)}, bf16[784,128]{1,0:T(8,128)(2,1)S(1)}, u32[]{:S(2)}, u32[]{:S(2)}) collective-permute-start(bf16[784,128]{1,0:T(8,128)(2,1)S(1)} %get-tuple-element.33.refs_0_), channel_id=1, source_target_pairs={{0,1},{1,0},{2,3},{3,2},{4,5},{5,4},{6,7},{7,6},{8,9},{9,8},{10,11... | collective-permute-start | bytes 602120 | tf_op jit(solution)/shard_map/ppermute | solution.py:256
  41.7 15.9 %collective-permute-start.2 = (bf16[784,128]{1,0:T(8,128)(2,1)S(1)}, bf16[784,128]{1,0:T(8,128)(2,1)S(1)}, u32[]{:S(2)}, u32[]{:S(2)}) collective-permute-start(bf16[784,128]{1,0:T(8,128)(2,1)S(1)} %get-tuple-element.33.refs_0_), channel_id=1, source_target_pairs={{0,2},{2,4},{4,6},{6,8},{8,10},{10,12},{12,14},{14,0},{1,3},{3,5},... | collective-permute-start | bytes 602120 | tf_op jit(solution)/shard_map/ppermute | solution.py:262
  43.4 14.2 %collective-permute-start.4 = (bf16[784,128]{1,0:T(8,128)(2,1)S(1)}, bf16[784,128]{1,0:T(8,128)(2,1)}, u32[]{:S(2)}, u32[]{:S(2)}) collective-permute-start(bf16[784,128]{1,0:T(8,128)(2,1)S(1)} %get-tuple-element.33.refs_0_), channel_id=1, source_target_pairs={{0,14},{2,0},{4,2},{6,4},{8,6},{10,8},{12,10},{14,12},{1,15},{3,1}... | collective-permute-start | bytes 602120 | tf_op jit(solution)/shard_map/ppermute | solution.py:262
  52.0 16.4 %copy-start.8 = (bf16[784,128]{1,0:T(8,128)(2,1)}, bf16[784,128]{1,0:T(8,128)(2,1)S(1)}, u32[]{:S(2)}) copy-start(bf16[784,128]{1,0:T(8,128)(2,1)S(1)} %collective-permute-done.6.refs_3_) | copy-start | bytes 602116
  52.0 9.7 %collective-permute-start.7 = (bf16[784,128]{1,0:T(8,128)(2,1)S(1)}, bf16[784,128]{1,0:T(8,128)(2,1)}, u32[]{:S(2)}, u32[]{:S(2)}) collective-permute-start(bf16[784,128]{1,0:T(8,128)(2,1)S(1)} %collective-permute-done.6.refs_3_), channel_id=1, source_target_pairs={{0,2},{2,4},{4,6},{6,8},{8,10},{10,12},{12,14},{14,0},{1,3},{3,5},... | collective-permute-start | bytes 602120 | tf_op jit(solution)/shard_map/ppermute | solution.py:262
  53.7 8.8 %collective-permute-start.9 = (bf16[784,128]{1,0:T(8,128)(2,1)S(1)}, bf16[784,128]{1,0:T(8,128)(2,1)}, u32[]{:S(2)}, u32[]{:S(2)}) collective-permute-start(bf16[784,128]{1,0:T(8,128)(2,1)S(1)} %collective-permute-done.6.refs_3_), channel_id=1, source_target_pairs={{0,14},{2,0},{4,2},{6,4},{8,6},{10,8},{12,10},{14,12},{1,15},{3,1}... | collective-permute-start | bytes 602120 | tf_op jit(solution)/shard_map/ppermute | solution.py:262
  57.6 13.2 %copy-start.10 = (bf16[784,128]{1,0:T(8,128)(2,1)}, bf16[784,128]{1,0:T(8,128)(2,1)S(1)}, u32[]{:S(2)}) copy-start(bf16[784,128]{1,0:T(8,128)(2,1)S(1)} %collective-permute-done.2.refs_1_) | copy-start | bytes 602116
  57.6 8.3 %collective-permute-start.3 = (bf16[784,128]{1,0:T(8,128)(2,1)S(1)}, bf16[784,128]{1,0:T(8,128)(2,1)S(1)}, u32[]{:S(2)}, u32[]{:S(2)}) collective-permute-start(bf16[784,128]{1,0:T(8,128)(2,1)S(1)} %collective-permute-done.2.refs_1_), channel_id=1, source_target_pairs={{0,2},{2,4},{4,6},{6,8},{8,10},{10,12},{12,14},{14,0},{1,3},{3,5},... | collective-permute-start | bytes 602120 | tf_op jit(solution)/shard_map/ppermute | solution.py:262
  57.6 10.8 %collective-permute-start.5 = (bf16[784,128]{1,0:T(8,128)(2,1)}, bf16[784,128]{1,0:T(8,128)(2,1)S(1)}, u32[]{:S(2)}, u32[]{:S(2)}) collective-permute-start(bf16[784,128]{1,0:T(8,128)(2,1)} %collective-permute-done.4.refs_2_), channel_id=1, source_target_pairs={{0,14},{2,0},{4,2},{6,4},{8,6},{10,8},{12,10},{14,12},{1,15},{3,1}... | collective-permute-start | bytes 602120 | tf_op jit(solution)/shard_map/ppermute | solution.py:262
  60.4 23.0 %collective-permute-start.11 = (bf16[2,1024,128]{2,1,0:T(8,128)(2,1)S(1)}, bf16[2,1024,128]{2,1,0:T(8,128)(2,1)S(1)}, u32[]{:S(2)}, u32[]{:S(2)}) collective-permute-start(bf16[2,1024,128]{2,1,0:T(8,128)(2,1)S(1)} %pad_maximum_fusion.refs_0_), channel_id=1, source_target_pairs={{0,128},{128,0},{1,129},{129,1},{2,130},{130,2},{3,131},{131,3},{4... | collective-permute-start | bytes 1572872 | tf_op jit(solution)/shard_map/ppermute | solution.py:286
  61.7 21.6 %collective-permute-start.12 = (bf16[2,1024,128]{2,1,0:T(8,128)(2,1)S(1)}, bf16[2,1024,128]{2,1,0:T(8,128)(2,1)S(1)}, u32[]{:S(2)}, u32[]{:S(2)}) collective-permute-start(bf16[2,1024,128]{2,1,0:T(8,128)(2,1)S(1)} %pad_maximum_fusion.refs_0_), channel_id=1, source_target_pairs={{0,32},{32,64},{64,96},{96,0},{1,33},{33,65},{65,97},{97,1},{2,34}... | collective-permute-start | bytes 1572872 | tf_op jit(solution)/shard_map/ppermute | solution.py:233
  62.5 20.8 %collective-permute-start.13 = (bf16[2,1024,128]{2,1,0:T(8,128)(2,1)S(1)}, bf16[2,1024,128]{2,1,0:T(8,128)(2,1)S(1)}, u32[]{:S(2)}, u32[]{:S(2)}) collective-permute-start(bf16[2,1024,128]{2,1,0:T(8,128)(2,1)S(1)} %pad_maximum_fusion.refs_0_), channel_id=1, source_target_pairs={{0,96},{32,0},{64,32},{96,64},{1,97},{33,1},{65,33},{97,65},{2,98}... | collective-permute-start | bytes 1572872 | tf_op jit(solution)/shard_map/ppermute | solution.py:233
  65.9 21.2 %collective-permute-start.23 = (bf16[8,256,128]{2,1,0:T(8,128)(2,1)S(1)}, bf16[8,256,128]{2,1,0:T(8,128)(2,1)S(1)}, u32[]{:S(2)}, u32[]{:S(2)}) collective-permute-start(bf16[8,256,128]{2,1,0:T(8,128)(2,1)S(1)} %all-to-all-done.1.refs_7_.refs_5_.refs_3_), channel_id=1, source_target_pairs={{0,16},{16,0},{1,17},{17,1},{2,18},{18,2},{3,19},{19,3},{4,20},{20... | collective-permute-start | bytes 1572872 | tf_op jit(solution)/shard_map/ppermute | solution.py:268
  68.5 6.9 %collective-permute-start.10 = (bf16[784,128]{1,0:T(8,128)(2,1)}, bf16[784,128]{1,0:T(8,128)(2,1)S(1)}, u32[]{:S(2)}, u32[]{:S(2)}) collective-permute-start(bf16[784,128]{1,0:T(8,128)(2,1)} %collective-permute-done.9.refs_5_), channel_id=1, source_target_pairs={{0,14},{2,0},{4,2},{6,4},{8,6},{10,8},{12,10},{14,12},{1,15},{3,1}... | collective-permute-start | bytes 602120 | tf_op jit(solution)/shard_map/ppermute | solution.py:262
  75.4 7.9 %collective-permute-start.8 = (bf16[784,128]{1,0:T(8,128)(2,1)}, bf16[784,128]{1,0:T(8,128)(2,1)S(1)}, u32[]{:S(2)}, u32[]{:S(2)}) collective-permute-start(bf16[784,128]{1,0:T(8,128)(2,1)} %collective-permute-done.7.refs_4_), channel_id=1, source_target_pairs={{0,2},{2,4},{4,6},{6,8},{8,10},{10,12},{12,14},{14,0},{1,3},{3,5},... | collective-permute-start | bytes 602120 | tf_op jit(solution)/shard_map/ppermute | solution.py:262
  83.3 0.8 copy-start.4
  84.2 28.2 %collective-permute-start.18 = (bf16[2,1024,128]{2,1,0:T(8,128)(2,1)S(1)}, bf16[2,1024,128]{2,1,0:T(8,128)(2,1)}, u32[]{:S(2)}, u32[]{:S(2)}) collective-permute-start(bf16[2,1024,128]{2,1,0:T(8,128)(2,1)S(1)} %collective-permute-done.12.refs_1_), channel_id=1, source_target_pairs={{0,32},{32,64},{64,96},{96,0},{1,33},{33,65},{65,97},{97,1},{2,34}... | collective-permute-start | bytes 1572872 | tf_op jit(solution)/shard_map/ppermute | solution.py:233
  84.2 28.2 %collective-permute-start.19 = (bf16[2,1024,128]{2,1,0:T(8,128)(2,1)S(1)}, bf16[2,1024,128]{2,1,0:T(8,128)(2,1)}, u32[]{:S(2)}, u32[]{:S(2)}) collective-permute-start(bf16[2,1024,128]{2,1,0:T(8,128)(2,1)S(1)} %collective-permute-done.11.refs_4_), channel_id=1, source_target_pairs={{0,32},{32,64},{64,96},{96,0},{1,33},{33,65},{65,97},{97,1},{2,34}... | collective-permute-start | bytes 1572872 | tf_op jit(solution)/shard_map/ppermute | solution.py:233
  85.2 27.1 %collective-permute-start.20 = (bf16[2,1024,128]{2,1,0:T(8,128)(2,1)S(1)}, bf16[2,1024,128]{2,1,0:T(8,128)(2,1)}, u32[]{:S(2)}, u32[]{:S(2)}) collective-permute-start(bf16[2,1024,128]{2,1,0:T(8,128)(2,1)S(1)} %collective-permute-done.11.refs_4_), channel_id=1, source_target_pairs={{0,96},{32,0},{64,32},{96,64},{1,97},{33,1},{65,33},{97,65},{2,98}... | collective-permute-start | bytes 1572872 | tf_op jit(solution)/shard_map/ppermute | solution.py:233
  87.0 16.6 %collective-permute-start.14 = (bf16[784,128]{1,0:T(8,128)(2,1)S(1)}, bf16[784,128]{1,0:T(8,128)(2,1)S(1)}, u32[]{:S(2)}, u32[]{:S(2)}) collective-permute-start(bf16[784,128]{1,0:T(8,128)(2,1)S(1)} %collective-permute-done.3.refs_0_), channel_id=1, source_target_pairs={{0,2},{2,4},{4,6},{6,8},{8,10},{10,12},{12,14},{14,0},{1,3},{3,5},... | collective-permute-start | bytes 602120 | tf_op jit(solution)/shard_map/ppermute | solution.py:262
  87.1 16.6 %collective-permute-start.15 = (bf16[784,128]{1,0:T(8,128)(2,1)S(1)}, bf16[784,128]{1,0:T(8,128)(2,1)S(1)}, u32[]{:S(2)}, u32[]{:S(2)}) collective-permute-start(bf16[784,128]{1,0:T(8,128)(2,1)S(1)} %collective-permute-done.5.refs_1_), channel_id=1, source_target_pairs={{0,14},{2,0},{4,2},{6,4},{8,6},{10,8},{12,10},{14,12},{1,15},{3,1}... | collective-permute-start | bytes 602120 | tf_op jit(solution)/shard_map/ppermute | solution.py:262
  89.7 3.4 %copy-start = (bf16[16,128,2048]{2,1,0:T(8,128)(2,1)S(1)}, bf16[16,128,2048]{2,1,0:T(8,128)(2,1)}, u32[]{:S(2)}) copy-start(bf16[16,128,2048]{2,1,0:T(8,128)(2,1)} %refs_2_.1) | copy-start | bytes 25165828
  93.1 0.9 copy-start.7
  94.0 0.9 copy-start.9
  95.0 0.9 copy-start.11
  95.9 10.4 %copy-start.1 = (bf16[16,128,2048]{2,1,0:T(8,128)(2,1)S(1)}, bf16[16,128,2048]{2,1,0:T(8,128)(2,1)}, u32[]{:S(2)}) copy-start(bf16[16,128,2048]{2,1,0:T(8,128)(2,1)} %refs_2_.1) | copy-start | bytes 25165828
  103.5 8.8 %collective-permute-start.16 = (bf16[784,128]{1,0:T(8,128)(2,1)S(1)}, bf16[784,128]{1,0:T(8,128)(2,1)S(1)}, u32[]{:S(2)}, u32[]{:S(2)}) collective-permute-start(bf16[784,128]{1,0:T(8,128)(2,1)S(1)} %collective-permute-done.8.refs_2_), channel_id=1, source_target_pairs={{0,2},{2,4},{4,6},{6,8},{8,10},{10,12},{12,14},{14,0},{1,3},{3,5},... | collective-permute-start | bytes 602120 | tf_op jit(solution)/shard_map/ppermute | solution.py:262
  103.6 8.7 %collective-permute-start.17 = (bf16[784,128]{1,0:T(8,128)(2,1)S(1)}, bf16[784,128]{1,0:T(8,128)(2,1)S(1)}, u32[]{:S(2)}, u32[]{:S(2)}) collective-permute-start(bf16[784,128]{1,0:T(8,128)(2,1)S(1)} %collective-permute-done.10.refs_3_), channel_id=1, source_target_pairs={{0,14},{2,0},{4,2},{6,4},{8,6},{10,8},{12,10},{14,12},{1,15},{3,1}... | collective-permute-start | bytes 602120 | tf_op jit(solution)/shard_map/ppermute | solution.py:262
  112.4 8.8 %collective-permute-start.21 = (bf16[784,128]{1,0:T(8,128)(2,1)S(1)}, bf16[784,128]{1,0:T(8,128)(2,1)S(1)}, u32[]{:S(2)}, u32[]{:S(2)}) collective-permute-start(bf16[784,128]{1,0:T(8,128)(2,1)S(1)} %collective-permute-done.14.refs_0_), channel_id=1, source_target_pairs={{0,2},{2,4},{4,6},{6,8},{8,10},{10,12},{12,14},{14,0},{1,3},{3,5},... | collective-permute-start | bytes 602120 | tf_op jit(solution)/shard_map/ppermute | solution.py:262
  112.5 8.7 %collective-permute-start.22 = (bf16[784,128]{1,0:T(8,128)(2,1)S(1)}, bf16[784,128]{1,0:T(8,128)(2,1)S(1)}, u32[]{:S(2)}, u32[]{:S(2)}) collective-permute-start(bf16[784,128]{1,0:T(8,128)(2,1)S(1)} %collective-permute-done.17.refs_3_), channel_id=1, source_target_pairs={{0,14},{2,0},{4,2},{6,4},{8,6},{10,8},{12,10},{14,12},{1,15},{3,1}... | collective-permute-start | bytes 602120 | tf_op jit(solution)/shard_map/ppermute | solution.py:262
  121.2 21.7 %copy-start.5 = (bf16[2,1024,128]{2,1,0:T(8,128)(2,1)S(1)}, bf16[2,1024,128]{2,1,0:T(8,128)(2,1)}, u32[]{:S(2)}) copy-start(bf16[2,1024,128]{2,1,0:T(8,128)(2,1)} %copy-done.4) | copy-start | bytes 1572868
  125.7 17.2 %collective-permute-start.24 = (bf16[512,1024]{1,0:T(8,128)(2,1)S(1)}, bf16[512,1024]{1,0:T(8,128)(2,1)S(1)}, u32[]{:S(2)}, u32[]{:S(2)}) collective-permute-start(bf16[512,1024]{1,0:T(8,128)(2,1)S(1)} %get-tuple-element.54), channel_id=1, source_target_pairs={{0,16},{16,0},{1,17},{17,1},{2,18},{18,2},{3,19},{19,3},{4,20},{20... | collective-permute-start | bytes 3145736 | tf_op jit(solution)/shard_map/ppermute | solution.py:302
  129.5 13.4 %collective-permute-start.25 = (bf16[2,1024,128]{2,1,0:T(8,128)(2,1)}, bf16[2,1024,128]{2,1,0:T(8,128)(2,1)S(1)}, u32[]{:S(2)}, u32[]{:S(2)}) collective-permute-start(bf16[2,1024,128]{2,1,0:T(8,128)(2,1)} %collective-permute-done.18.refs_2_), channel_id=1, source_target_pairs={{0,128},{128,0},{1,129},{129,1},{2,130},{130,2},{3,131},{131,3},{4... | collective-permute-start | bytes 1572872 | tf_op jit(solution)/shard_map/ppermute | solution.py:298
  146.7 3.6 %collective-permute-start.26 = (bf16[8,512,128]{2,1,0:T(8,128)(2,1)S(1)}, bf16[8,512,128]{2,1,0:T(8,128)(2,1)S(1)}, u32[]{:S(2)}, u32[]{:S(2)}) collective-permute-start(bf16[8,512,128]{2,1,0:T(8,128)(2,1)S(1)} %get-tuple-element.60), channel_id=1, source_target_pairs={{0,16},{16,0},{1,17},{17,1},{2,18},{18,2},{3,19},{19,3},{4,20},{20... | collective-permute-start | bytes 3145736 | tf_op jit(solution)/shard_map/ppermute | solution.py:304

commit v2 on v1

v2 whole, which is shorter than its diff:
```python
import jax
import jax.numpy as jnp
from jax import lax
from jax.experimental import pallas as pl
from jax.experimental.pallas import tpu as pltpu
from jax.sharding import Mesh
from jax.sharding import PartitionSpec as P

P_SIZE = 32768
ROW = ("yl", "x", "c")
CHIPS = ("yl", "x")
COL = ("z", "yh")
F32 = jnp.float32
BF16 = jnp.bfloat16
PAY = 784
LIMIT = pltpu.CompilerParams(vmem_limit_bytes=16 * 1024 * 1024)
VM = pl.BlockSpec(memory_space=pltpu.VMEM)
SM = pl.BlockSpec(memory_space=pltpu.SMEM)
HB = pl.BlockSpec(memory_space=pltpu.HBM)


def swap():
    return [(0, 1), (1, 0)]


def ring(size, step):
    return [(i, (i + step) % size) for i in range(size)]


def dot(a, b, dims):
    return lax.dot_general(a, b, (dims, ((), ())), preferred_element_type=F32)


def cost(flops, moved):
    return pl.CostEstimate(flops=flops, transcendentals=0, bytes_accessed=moved)


def encode_kernel(mine, got, stacked, other, out):
    def step(j, _):
        rows = jnp.concatenate([mine[j], got[j]], axis=1)
        x_side = jnp.concatenate([stacked[0:256], other[0:256]], axis=1)
        out[j, :, 0:128] = dot(x_side, rows, ((1,), (1,))).astype(BF16)
        for w in range(2):
            here = slice(256 * (w + 1), 256 * (w + 2))
            side = jnp.concatenate([stacked[here], other[here]], axis=1)
            theta = dot(rows, side, ((1,), (1,))).astype(BF16)
            for h in range(2):
                lanes = slice(128 * (w + 1), 128 * (w + 2))
                out[j, 128 * h:128 * (h + 1), lanes] = theta[:, 128 * h:128 * (h + 1)]
        return 0

    lax.fori_loop(0, 8, step, 0, unroll=2)


def encode(*args):
    return pl.pallas_call(
        encode_kernel,
        in_specs=[VM] * 4,
        out_specs=VM,
        out_shape=jax.ShapeDtypeStruct((8, 256, 384), BF16),
        compiler_params=LIMIT,
        cost_estimate=cost(2 * 1024 * 256 * 768, 3 << 20),
        name="encode",
    )(*args)


def own_kernel(parts, out, spread):
    total = parts[0].astype(F32)
    for j in range(1, 8):
        total = total + parts[j].astype(F32)
    total = jnp.concatenate([total[:, 128 * n:128 * (n + 1)] for n in range(3)], axis=0).astype(BF16)
    out[0:768] = total
    for j in range(8):
        spread[j] = total[0:256]
    wide = total.astype(F32)
    rows = []
    for w in range(2):
        at = 256 * (w + 1)
        acc = jnp.sum(wide[0:128] * wide[at:at + 128].T, axis=0, keepdims=True)
        acc = acc + jnp.sum(wide[128:256] * wide[at + 128:at + 256].T, axis=0, keepdims=True)
        rows.append(acc)
    rows.append(jnp.zeros((14, 128), F32))
    out[768:784] = jnp.concatenate(rows, axis=0).astype(BF16)


def own_points(parts):
    return pl.pallas_call(
        own_kernel,
        in_specs=[VM],
        out_specs=[VM, VM],
        out_shape=[jax.ShapeDtypeStruct((PAY, 128), BF16), jax.ShapeDtypeStruct((8, 256, 128), BF16)],
        compiler_params=LIMIT,
        cost_estimate=cost(1 << 24, 2 << 20),
        name="own",
    )(parts)


def make_exchange_kernel(shapes, where, first, last):
    def kernel(pos, *refs):
        held = refs[:len(shapes)]
        pays = []
        for ref, shape in zip(held, shapes):
            pays += [ref] if len(shape) == 2 else [ref.at[0], ref.at[1]]
        kern, same, cross = refs[len(shapes):len(shapes) + 3]
        rest = refs[len(shapes) + 3:]
        if not first:
            e_in, u_in = rest[:2]
            rest = rest[2:]
        v_buf, sems = rest[-2:]
        rest = rest[:-2]
        flag = pos[0] == 0

        def fetch(h, b):
            lanes = pl.ds(pl.multiple_of(512 * h, 512), 512)
            return pltpu.make_async_copy(
                kern.at[pos[1 + where[b]], :, lanes], v_buf.at[h, pl.ds(128 * b, 128)], sems.at[h, b]
            )

        for h in range(4):
            for b in range(len(where)):
                fetch(h, b).start()

        def theta(w):
            at = 256 * (w + 1)
            return jnp.concatenate(
                [jnp.concatenate([p[at:at + 128], p[at + 128:at + 256]], axis=1) for p in pays], axis=0
            )

        def pair_step(h, _):
            for b in range(len(where)):
                fetch(h, b).wait()
            for half in range(2):
                chip_step(h, half)
            return 0

        def chip_step(h, half):
            chip = 2 * h + half
            xp = jnp.concatenate([p[0:256] for p in pays], axis=1)
            dens = jnp.concatenate([p[768:784] for p in pays], axis=1)
            lanes = pl.ds(pl.multiple_of(256 * chip, 256), 256)
            a = same[chip]
            b = cross[chip]
            xq = jnp.concatenate([jnp.where(flag, a, b), jnp.where(flag, b, a)], axis=1)
            v = v_buf[h, :, 256 * half:256 * (half + 1)]
            u = dot(dens, v, ((1,), (0,)))
            if not first:
                u = u + u_in[:, lanes]
            if not last:
                rest[1][:, lanes] = u
            wide = v.astype(F32)
            for w in range(2):
                tile = dot(theta(w), xq, ((1,), (0,)))
                amp = (wide * tile).astype(BF16)
                e = dot(xp, amp, ((1,), (0,)))
                rows = slice(256 * w, 256 * (w + 1))
                if not first:
                    e = e + e_in[rows, lanes]
                if not last:
                    rest[0][rows, lanes] = e
                else:
                    f = (u[w:w + 1] * xq.astype(F32) - e).astype(BF16)
                    here = pl.ds(pl.multiple_of(128 * chip, 128), 128)
                    low, high = f[:, 0:128], f[:, 128:256]
                    rest[0][rows, here] = jnp.where(flag, low, high)
                    rest[1][rows, here] = jnp.where(flag, high, low)

        lax.fori_loop(0, 4, pair_step, 0)

    return kernel


def exchange(pos, held, where, coulomb, same, cross, totals, last):
    first = totals is None
    args = [pos, *held, coulomb, same, cross]
    in_specs = [SM] + [VM] * len(held) + [HB, VM, VM]
    alias = {}
    if not first:
        if not last:
            alias = {len(args): 0, len(args) + 1: 1}
        args += list(totals)
        in_specs += [VM, VM]
    if last:
        out_shape = [jax.ShapeDtypeStruct((512, 1024), BF16)] * 2
    else:
        out_shape = [jax.ShapeDtypeStruct((512, 2048), F32), jax.ShapeDtypeStruct((16, 2048), F32)]
    rows = 128 * len(where)
    return pl.pallas_call(
        make_exchange_kernel([a.shape for a in held], where, first, last),
        in_specs=in_specs,
        out_specs=[VM, VM],
        out_shape=out_shape,
        scratch_shapes=[pltpu.VMEM((4, rows, 512), BF16), pltpu.SemaphoreType.DMA((4, len(where)))],
        input_output_aliases=alias,
        compiler_params=LIMIT,
        cost_estimate=cost(8 * rows * 2048 * 256, 8 << 20),
        name="exchange",
    )(*args)


def decode_kernel(pos, f_mine, f_got, *refs):
    cols = refs[:8]
    keep, give = refs[8:]
    f = (f_mine[...].astype(F32) + f_got[...].astype(F32)).astype(BF16)
    for j in range(8):
        chip = lax.bitwise_xor(pos[17], j // 4) * 4 + lax.rem(pos[18] - j % 4 + 4, 4)
        g = dot(f, jnp.concatenate([cols[j][0], cols[j][1]], axis=1), ((1,), (0,)))
        keep[chip] = g[:, 0:128].astype(BF16)
        give[chip] = g[:, 128:256].astype(BF16)


def decode(pos, f, f_got, cols):
    return pl.pallas_call(
        decode_kernel,
        in_specs=[SM] + [VM] * 10,
        out_specs=[VM, VM],
        out_shape=[jax.ShapeDtypeStruct((8, 512, 128), BF16)] * 2,
        compiler_params=LIMIT,
        cost_estimate=cost(2 * 512 * 1024 * 2048, 8 << 20),
        name="decode",
    )(pos, f, f_got, *cols)


def sum_kernel(parts, out):
    total = parts[0].astype(F32)
    for j in range(1, 8):
        total = total + parts[j].astype(F32)
    total = total.astype(BF16)
    for w in range(2):
        for c in range(16):
            out[c, w] = total[256 * w + 16 * c:256 * w + 16 * (c + 1)]


def program(collocation, greens, trial_orbitals, coulomb):
    yl, x, c = lax.axis_index("yl"), lax.axis_index("x"), lax.axis_index("c")
    z, yh = lax.axis_index("z"), lax.axis_index("yh")

    def place(step, flip):
        return lax.rem(z - step + 8, 8) * 2 + (yh if flip == 0 else 1 - yh)

    order = [(0, 0), (0, 1)]
    for s in (1, 2, 3):
        order += [(s, 0), (s, 1), (-s, 0), (-s, 1)]
    order += [(4, 0), (-4, 1)]
    pos = jnp.stack([c] + [place(*k) for k in order] + [yl, x]).astype(jnp.int32)

    coulomb = pltpu.with_memory_space_constraint(coulomb, pltpu.HBM)
    halves = collocation.reshape(8, 2, 128, 128)
    mine = lax.dynamic_index_in_dim(halves, c, 1, keepdims=False)
    give = lax.dynamic_index_in_dim(halves, 1 - c, 1, keepdims=False)
    stacked = jnp.concatenate([trial_orbitals, greens.reshape(512, 128)], axis=0)
    got = lax.ppermute(give, "c", swap())
    other = lax.ppermute(stacked, "c", swap())
    partial_value = encode(mine, got, stacked, other)
    parts = lax.all_to_all(partial_value, CHIPS, 0, 0, tiled=True)
    own, spread = own_points(parts)

    mate = lax.ppermute(own, "yh", swap())
    pair = jnp.stack([own, mate])
    same = lax.all_to_all(spread, CHIPS, 0, 0, tiled=True)
    cross = lax.ppermute(same, "c", swap())
    up, down = [pair], [pair]
    for _ in range(3):
        up.append(lax.ppermute(up[-1], "z", ring(8, 1)))
        down.append(lax.ppermute(down[-1], "z", ring(8, -1)))
    last_up, last_down = up[3][0], down[3][1]
    far_up = lax.ppermute(last_up, "z", ring(8, 1))
    far_down = lax.ppermute(last_down, "z", ring(8, -1))
    far = [far_up, far_down]
    base = jnp.stack([mine.reshape(1024, 128), got.reshape(1024, 128)])
    base, _ = lax.optimization_barrier((base, pair))
    cols = [base] + [None] * 7
    cols[4] = lax.ppermute(base, "yl", swap())
    cols[1] = lax.ppermute(base, "x", ring(4, 1))
    cols[3] = lax.ppermute(base, "x", ring(4, -1))
    cols[2] = lax.ppermute(cols[1], "x", ring(4, 1))
    cols[7] = lax.ppermute(cols[4], "x", ring(4, -1))
    cols[5] = lax.ppermute(cols[4], "x", ring(4, 1))
    cols[6] = lax.ppermute(cols[2], "yl", swap())
    totals = exchange(pos, [pair, up[1], down[1]], list(range(6)), coulomb, same, cross, None, False)
    totals = exchange(pos, [up[2], down[2]], [6, 7, 8, 9], coulomb, same, cross, totals, False)
    f_mine, f_give = exchange(pos, [up[3], down[3], *far], [10, 11, 12, 13, 14, 15], coulomb, same, cross, totals, True)
    f_got = lax.ppermute(f_give, "c", swap())
    keep, send = decode(pos, f_mine, f_got, cols)
    back = lax.ppermute(send, "c", swap())
    both = (keep.astype(F32) + back.astype(F32)).astype(BF16)
    terms = lax.all_to_all(both, CHIPS, 0, 0, tiled=True)
    summed = pl.pallas_call(
        sum_kernel,
        in_specs=[VM],
        out_specs=VM,
        out_shape=jax.ShapeDtypeStruct((16, 2, 16, 128), BF16),
        compiler_params=LIMIT,
        name="chip_sum",
    )(terms)
    shares = lax.all_to_all(summed.reshape(16, 32, 128), COL, 0, 0, tiled=True).reshape(16, 2, 16, 128)
    total = jnp.sum(shares.astype(F32), axis=0) * P_SIZE ** (-0.5)
    return jnp.swapaxes(total, 0, 1).astype(BF16)


def solution(mesh):
    finer = Mesh(mesh.devices.reshape(2, 4, 2, 8, 2), ("yl", "x", "c", "z", "yh"))
    placed = (P(COL, ROW), P(None, None, ROW), P(None, ROW), P(None, ROW, COL))
    return jax.shard_map(program, mesh=finer, in_specs=placed, out_specs=P(COL, None, ROW), check_vma=False)
```

time: 187 us -> 168 us (0.90)
  starting transfers between devices: 49.5 us -> 40.3 us
  local copies, waits for them, and re-layouts: 10.5 us -> 3.53 us
  Pallas kernels: 30.4 us -> 27.7 us
    ppermute x27 -> x21, starting transfers between devices: 46 us -> 36.8 us  [the longest x3 12.9 us: program(): down.append(lax.ppermute(down[-1], 'z', ring(8, -1)))]
    unnamed x24 -> x4, local copies, waits for them, and re-layouts: 8.75 us -> 1.74 us
    all_to_all x1, waiting for transfers between devices: 0.01 us -> 3 us  [program(): same = lax.all_to_all(spread, CHIPS, 0, 0, tiled=True)]
    ppermute x27 -> x21, waiting for transfers between devices: 34.8 us -> 32 us  [the longest x1 9.07 us: program(): cols[7] = lax.ppermute(cols[4], 'x', ring(4, -1))]
    pallas_call x6 -> x5, Pallas kernels: 25.6 us -> 23.1 us  [the longest x3 21.7 us: exchange(): pl.pallas_call(make_exchange_kernel([a.shape for a in held], where, first...]
  transfers between devices with their start and end apart: 28 -> 22, of which waited for: 8 -> 9; matrix products, arithmetic and copies ran while one was open for 1% -> 1% of each run, Pallas kernels for 11% -> 13%
where the time goes in v2:
time: 168 us; the launch traced here: 167 us
  blocking collectives  59.5 us (35%)
  starting transfers between devices  40.3 us (24%)
  waiting for transfers between devices  35 us (21%)
  Pallas kernels  27.7 us (16%)
  local copies, waits for them, and re-layouts  3.53 us (2%)
    all_to_all x1, blocking collectives, program(): parts = lax.all_to_all(partial_value, CHIPS, 0, 0, tiled=True)  24.6 us
    pallas_call x3, Pallas kernels, exchange(): pl.pallas_call(make_exchange_kernel([a.shape for a in held], where, first...  21.7 us
    all_to_all x1, blocking collectives, program(): terms = lax.all_to_all(both, CHIPS, 0, 0, tiled=True)  19.5 us
    all_to_all x1, blocking collectives, program(): lax.all_to_all(summed.reshape(16, 32, 128), COL, 0, 0, tiled=True)  15.3 us
    ppermute x3, starting transfers between devices, program(): down.append(lax.ppermute(down[-1], 'z', ring(8, -1)))  12.9 us
    ppermute x1, waiting for transfers between devices, program(): cols[7] = lax.ppermute(cols[4], 'x', ring(4, -1))  9.07 us
    ppermute x1, waiting for transfers between devices, program(): cols[3] = lax.ppermute(base, 'x', ring(4, -1))  8.58 us
    ppermute x3, waiting for transfers between devices, program(): down.append(lax.ppermute(down[-1], 'z', ring(8, -1)))  7.33 us
  transfers between devices with their start and end apart: 22, of which 9 were waited for; matrix products, arithmetic and copies ran while one was open for 1% of the time, Pallas kernels for 13%

profile of v2, /device:TPU:1, one launch (start us, length us, event | category | flops | bytes accessed | tf_op | source)
XLA Modules:
  0.0 167.4 jit_solution(18295742278847548526)
XLA Ops:
  0.0 1.1 dynamic-slice_bitcast_fusion
  1.1 3.3 %collective-permute-start = (bf16[8,128,128]{2,1,0:T(8,128)(2,1)S(1)}, bf16[8,128,128]{2,1,0:T(8,128)(2,1)S(1)}, u32[]{:S(2)}, u32[]{:S(2)}) collective-permute-start(bf16[8,128,128]{2,1,0:T(8,128)(2,1)S(1)} %get-tuple-element.27), channel_id=1, source_target_pairs={{0,16},{16,0},{1,17},{17,1},{2,18},{18,2},{3,19},{19,3},{4,20},{20... | collective-permute-start | bytes 786440 | tf_op jit(solution)/shard_map/ppermute | solution.py:251
  4.4 0.9 pad_maximum_fusion.2.stacked
  5.3 0.1 collective-permute-start.1
  5.4 1.4 collective-permute-done.1.other
  6.8 0.0 collective-permute-done.got
  6.8 1.3 encode.1
  8.1 24.6 %all_to_all.20.parts = bf16[8,256,384]{2,1,0:T(8,128)(2,1)S(1)} all-to-all(bf16[8,256,384]{2,1,0:T(8,128)(2,1)S(1)} %encode.1), channel_id=1, replica_groups=mesh['yl'=2,'x'=4,'c'=2,'z'=8,'yh'=2] {'yl','x'}, dimensions={0} | all-to-all | bytes 3145728 | tf_op jit(solution)/shard_map/all_to_all | solution.py:254
  32.7 1.0 own.1
  33.8 2.6 %collective-permute-start.2 = (bf16[784,128]{1,0:T(8,128)(2,1)S(1)}, bf16[784,128]{1,0:T(8,128)(2,1)S(1)}, u32[]{:S(2)}, u32[]{:S(2)}) collective-permute-start(bf16[784,128]{1,0:T(8,128)(2,1)S(1)} %get-tuple-element.16), channel_id=1, source_target_pairs={{0,1},{1,0},{2,3},{3,2},{4,5},{5,4},{6,7},{7,6},{8,9},{9,8},{10,11... | collective-permute-start | bytes 602120 | tf_op jit(solution)/shard_map/ppermute | solution.py:257
  36.4 3.5 %all-to-all-start.1 = ((bf16[8,256,128]{2,1,0:T(8,128)(2,1)}), bf16[8,256,128]{2,1,0:T(8,128)(2,1)S(1)}, u32[]{:S(2)}, u32[]{:S(2)}) async-start(bf16[8,256,128]{2,1,0:T(8,128)(2,1)} %get-tuple-element.17), calls=%async_computation.1 | async-start | bytes 1048576 | tf_op jit(solution)/shard_map/all_to_all | solution.py:259
  39.9 1.1 collective-permute-done.2
  41.1 5.7 %collective-permute-start.6 = (bf16[2,784,128]{2,1,0:T(8,128)(2,1)S(1)}, bf16[2,784,128]{2,1,0:T(8,128)(2,1)S(1)}, u32[]{:S(2)}, u32[]{:S(2)}) collective-permute-start(bf16[2,784,128]{2,1,0:T(8,128)(2,1)S(1)} %pad_maximum_fusion.1.refs_0_), channel_id=1, source_target_pairs={{0,14},{2,0},{4,2},{6,4},{8,6},{10,8},{12,10},{14,12},{1,15},{3,1}... | collective-permute-start | bytes 1204232 | tf_op jit(solution)/shard_map/ppermute | solution.py:264
  46.7 0.1 pad_maximum_fusion.refs_0_
  46.8 0.3 collective-permute-start.13
  47.1 3.0 %all-to-all-done.1.refs_4_.refs_3_.refs_5_ = bf16[8,256,128]{2,1,0:T(8,128)(2,1)S(1)} async-done(((bf16[8,256,128]{2,1,0:T(8,128)(2,1)}), bf16[8,256,128]{2,1,0:T(8,128)(2,1)S(1)}, u32[]{:S(2)}, u32[]{:S(2)}) %all-to-all-start.1) | async-done | bytes 524320 | tf_op jit(solution)/shard_map/all_to_all | solution.py:259
  50.1 0.8 collective-permute-start.11
  50.9 2.2 %collective-permute-done.6.refs_2_ = bf16[2,784,128]{2,1,0:T(8,128)(2,1)S(1)} collective-permute-done((bf16[2,784,128]{2,1,0:T(8,128)(2,1)S(1)}, bf16[2,784,128]{2,1,0:T(8,128)(2,1)S(1)}, u32[]{:S(2)}, u32[]{:S(2)}) %collective-permute-start.6) | collective-permute-done | bytes 401440 | tf_op jit(solution)/shard_map/ppermute | solution.py:264
  53.1 3.7 %collective-permute-start.7 = (bf16[2,784,128]{2,1,0:T(8,128)(2,1)S(1)}, bf16[2,784,128]{2,1,0:T(8,128)(2,1)S(1)}, u32[]{:S(2)}, u32[]{:S(2)}) collective-permute-start(bf16[2,784,128]{2,1,0:T(8,128)(2,1)S(1)} %collective-permute-done.6.refs_2_), channel_id=1, source_target_pairs={{0,14},{2,0},{4,2},{6,4},{8,6},{10,8},{12,10},{14,12},{1,15},{3,1}... | collective-permute-start | bytes 1204232 | tf_op jit(solution)/shard_map/ppermute | solution.py:264
  56.8 0.7 copy-done
  57.6 0.0 collective-permute-done.3.refs_1_
  57.6 5.1 %collective-permute-done.7.refs_1_ = bf16[2,784,128]{2,1,0:T(8,128)(2,1)S(1)} collective-permute-done((bf16[2,784,128]{2,1,0:T(8,128)(2,1)S(1)}, bf16[2,784,128]{2,1,0:T(8,128)(2,1)S(1)}, u32[]{:S(2)}, u32[]{:S(2)}) %collective-permute-start.7) | collective-permute-done | bytes 401440 | tf_op jit(solution)/shard_map/ppermute | solution.py:264
  62.7 3.5 %collective-permute-start.8 = (bf16[2,784,128]{2,1,0:T(8,128)(2,1)S(1)}, bf16[2,784,128]{2,1,0:T(8,128)(2,1)S(1)}, u32[]{:S(2)}, u32[]{:S(2)}) collective-permute-start(bf16[2,784,128]{2,1,0:T(8,128)(2,1)S(1)} %collective-permute-done.7.refs_1_), channel_id=1, source_target_pairs={{0,14},{2,0},{4,2},{6,4},{8,6},{10,8},{12,10},{14,12},{1,15},{3,1}... | collective-permute-start | bytes 1204232 | tf_op jit(solution)/shard_map/ppermute | solution.py:264
  66.2 0.1 stack.91.pos
  66.3 1.0 collective-permute-start.16
  67.3 1.6 collective-permute-start.14
  68.9 1.0 copy-done.1
  69.9 7.9 %exchange.3 = (f32[512,2048]{1,0:T(8,128)S(1)}, f32[16,2048]{1,0:T(8,128)S(1)}) custom-call(s32[19]{0:T(128)S(1)} %stack.91.pos, bf16[2,784,128]{2,1,0:T(8,128)(2,1)S(1)} %pad_maximum_fusion.1.refs_0_, bf16[2,784,128]{2,1,0:T(8,128)(2,1)} %collective-permute-done.3.refs_1_, bf16[2,784,128]{2,1,0:T(8,128)(2,1)S(1)} %copy-done.1, ...), custom_call_target="tpu_custom_call" | custom-call | flops 3221225472 | bytes 8388608 | tf_op jit(solution)/shard_map/exchange/pallas_call | solution.py:187
  77.8 2.7 %collective-permute-start.10 = (bf16[784,128]{1,0:T(8,128)(2,1)S(1)}, bf16[784,128]{1,0:T(8,128)(2,1)S(1)}, u32[]{:S(2)}, u32[]{:S(2)}) collective-permute-start(bf16[784,128]{1,0:T(8,128)(2,1)S(1)} %slice_bitcast_fusion), channel_id=1, source_target_pairs={{0,14},{2,0},{4,2},{6,4},{8,6},{10,8},{12,10},{14,12},{1,15},{3,1}... | collective-permute-start | bytes 602120 | tf_op jit(solution)/shard_map/ppermute | solution.py:267
  80.6 0.3 collective-permute-start.9
  80.9 6.1 %exchange.4 = (f32[512,2048]{1,0:T(8,128)S(1)}, f32[16,2048]{1,0:T(8,128)S(1)}) custom-call(s32[19]{0:T(128)S(1)} %stack.91.pos, bf16[2,784,128]{2,1,0:T(8,128)(2,1)S(1)} %collective-permute-done.4.refs_0_, bf16[2,784,128]{2,1,0:T(8,128)(2,1)S(1)} %collective-permute-done.7.refs_1_, ...), custom_call_target="tpu_custom_call", output_to_operand_aliasing={{0}: (6, {}), {1}: (7, {})} | custom-call | flops 2147483648 | bytes 8388608 | tf_op jit(solution)/shard_map/exchange/pallas_call | solution.py:187
  87.0 7.6 %exchange.5 = (bf16[512,1024]{1,0:T(8,128)(2,1)S(1)}, bf16[512,1024]{1,0:T(8,128)(2,1)S(1)}) custom-call(s32[19]{0:T(128)S(1)} %stack.91.pos, bf16[2,784,128]{2,1,0:T(8,128)(2,1)S(1)} %collective-permute-done.5.refs_0_, bf16[2,784,128]{2,1,0:T(8,128)(2,1)S(1)} %collective-permute-done.8.refs_1_, bf16[784,128]{1,0:T(8,128)(2,1)S(1)} %collective-permute-done.9.refs_2_, ...), custom_call_target="tpu_custom_call" | custom-call | flops 3221225472 | bytes 8388608 | tf_op jit(solution)/shard_map/exchange/pallas_call | solution.py:187
  94.7 5.3 %collective-permute-start.12 = (bf16[512,1024]{1,0:T(8,128)(2,1)S(1)}, bf16[512,1024]{1,0:T(8,128)(2,1)S(1)}, u32[]{:S(2)}, u32[]{:S(2)}) collective-permute-start(bf16[512,1024]{1,0:T(8,128)(2,1)S(1)} %get-tuple-element.23), channel_id=1, source_target_pairs={{0,16},{16,0},{1,17},{17,1},{2,18},{18,2},{3,19},{19,3},{4,20},{20... | collective-permute-start | bytes 3145736 | tf_op jit(solution)/shard_map/ppermute | solution.py:282
  100.0 1.2 collective-permute-start.15
  101.2 0.2 collective-permute-start.17
  101.5 2.4 %collective-permute-start.19 = (bf16[2,1024,128]{2,1,0:T(8,128)(2,1)S(1)}, bf16[2,1024,128]{2,1,0:T(8,128)(2,1)S(1)}, u32[]{:S(2)}, u32[]{:S(2)}) collective-permute-start(bf16[2,1024,128]{2,1,0:T(8,128)(2,1)S(1)} %collective-permute-done.16.refs_4_), channel_id=1, source_target_pairs={{0,96},{32,0},{64,32},{96,64},{1,97},{33,1},{65,33},{97,65},{2,98}... | collective-permute-start | bytes 1572872 | tf_op jit(solution)/shard_map/ppermute | solution.py:276
  103.9 0.9 collective-permute-start.18
  104.8 8.6 %collective-permute-done.15.refs_3_ = bf16[2,1024,128]{2,1,0:T(8,128)(2,1)S(1)} collective-permute-done((bf16[2,1024,128]{2,1,0:T(8,128)(2,1)S(1)}, bf16[2,1024,128]{2,1,0:T(8,128)(2,1)S(1)}, u32[]{:S(2)}, u32[]{:S(2)}) %collective-permute-start.15) | collective-permute-done | bytes 524320 | tf_op jit(solution)/shard_map/ppermute | solution.py:274
  113.4 2.2 %collective-permute-done.17.refs_5_ = bf16[2,1024,128]{2,1,0:T(8,128)(2,1)S(1)} collective-permute-done((bf16[2,1024,128]{2,1,0:T(8,128)(2,1)S(1)}, bf16[2,1024,128]{2,1,0:T(8,128)(2,1)S(1)}, u32[]{:S(2)}, u32[]{:S(2)}) %collective-permute-start.17) | collective-permute-done | bytes 524320 | tf_op jit(solution)/shard_map/ppermute | solution.py:277
  115.5 9.1 %collective-permute-done.19.refs_7_ = bf16[2,1024,128]{2,1,0:T(8,128)(2,1)S(1)} collective-permute-done((bf16[2,1024,128]{2,1,0:T(8,128)(2,1)S(1)}, bf16[2,1024,128]{2,1,0:T(8,128)(2,1)S(1)}, u32[]{:S(2)}, u32[]{:S(2)}) %collective-permute-start.19) | collective-permute-done | bytes 524320 | tf_op jit(solution)/shard_map/ppermute | solution.py:276
  124.6 3.5 %decode.1 = (bf16[8,512,128]{2,1,0:T(8,128)(2,1)S(1)}, bf16[8,512,128]{2,1,0:T(8,128)(2,1)S(1)}) custom-call(s32[19]{0:T(128)S(1)} %stack.91.pos, bf16[512,1024]{1,0:T(8,128)(2,1)S(1)} %get-tuple-element.22.f_mine, bf16[512,1024]{1,0:T(8,128)(2,1)S(1)} %collective-permute-done.12.f_got, bf16[2,1024,128]{2,1,0:T(8,128)(2,1)S(1)} %pad_maximum_fusion.refs_0_, ...), custom_call_target="tpu_custom_call" | custom-call | flops 2147483648 | bytes 8388608 | tf_op jit(solution)/shard_map/decode/pallas_call | solution.py:212
  128.1 1.0 collective-permute-start.20
  129.2 2.3 %collective-permute-done.20 = bf16[8,512,128]{2,1,0:T(8,128)(2,1)S(1)} collective-permute-done((bf16[8,512,128]{2,1,0:T(8,128)(2,1)S(1)}, bf16[8,512,128]{2,1,0:T(8,128)(2,1)S(1)}, u32[]{:S(2)}, u32[]{:S(2)}) %collective-permute-start.20) | collective-permute-done | bytes 1048608 | tf_op jit(solution)/shard_map/ppermute | solution.py:284
  131.5 0.3 add_convert_fusion
  131.7 19.5 %all_to_all.21.parts = bf16[8,512,128]{2,1,0:T(8,128)(2,1)S(1)} all-to-all(bf16[8,512,128]{2,1,0:T(8,128)(2,1)S(1)} %add_convert_fusion), channel_id=1, replica_groups=mesh['yl'=2,'x'=4,'c'=2,'z'=8,'yh'=2] {'yl','x'}, dimensions={0} | all-to-all | bytes 2097152 | tf_op jit(solution)/shard_map/all_to_all | solution.py:286
  151.3 0.1 chip_sum.1
  151.4 15.3 %all_to_all.22 = bf16[16,32,128]{2,1,0:T(8,128)(2,1)S(1)} all-to-all(bf16[16,32,128]{2,1,0:T(8,128)(2,1)S(1)} %bitcast.44), channel_id=1, replica_groups=mesh['yl'=2,'x'=4,'c'=2,'z'=8,'yh'=2] {'z','yh'}, dimensions={0} | all-to-all | bytes 262144 | tf_op jit(solution)/shard_map/all_to_all | solution.py:295
  166.8 0.6 copy.11
  (21 shorter events, 0.1 us)
Async XLA Ops:
  1.1 5.7 %collective-permute-start = (bf16[8,128,128]{2,1,0:T(8,128)(2,1)S(1)}, bf16[8,128,128]{2,1,0:T(8,128)(2,1)S(1)}, u32[]{:S(2)}, u32[]{:S(2)}) collective-permute-start(bf16[8,128,128]{2,1,0:T(8,128)(2,1)S(1)} %get-tuple-element.27), channel_id=1, source_target_pairs={{0,16},{16,0},{1,17},{17,1},{2,18},{18,2},{3,19},{19,3},{4,20},{20... | collective-permute-start | bytes 786440 | tf_op jit(solution)/shard_map/ppermute | solution.py:251
  5.3 1.5 collective-permute-start.1
  33.8 7.2 %collective-permute-start.2 = (bf16[784,128]{1,0:T(8,128)(2,1)S(1)}, bf16[784,128]{1,0:T(8,128)(2,1)S(1)}, u32[]{:S(2)}, u32[]{:S(2)}) collective-permute-start(bf16[784,128]{1,0:T(8,128)(2,1)S(1)} %get-tuple-element.16), channel_id=1, source_target_pairs={{0,1},{1,0},{2,3},{3,2},{4,5},{5,4},{6,7},{7,6},{8,9},{9,8},{10,11... | collective-permute-start | bytes 602120 | tf_op jit(solution)/shard_map/ppermute | solution.py:257
  36.4 13.7 %all-to-all-start.1 = ((bf16[8,256,128]{2,1,0:T(8,128)(2,1)}), bf16[8,256,128]{2,1,0:T(8,128)(2,1)S(1)}, u32[]{:S(2)}, u32[]{:S(2)}) async-start(bf16[8,256,128]{2,1,0:T(8,128)(2,1)} %get-tuple-element.17), calls=%async_computation.1 | async-start | bytes 1048576 | tf_op jit(solution)/shard_map/all_to_all | solution.py:259
  41.1 12.0 %collective-permute-start.6 = (bf16[2,784,128]{2,1,0:T(8,128)(2,1)S(1)}, bf16[2,784,128]{2,1,0:T(8,128)(2,1)S(1)}, u32[]{:S(2)}, u32[]{:S(2)}) collective-permute-start(bf16[2,784,128]{2,1,0:T(8,128)(2,1)S(1)} %pad_maximum_fusion.1.refs_0_), channel_id=1, source_target_pairs={{0,14},{2,0},{4,2},{6,4},{8,6},{10,8},{12,10},{14,12},{1,15},{3,1}... | collective-permute-start | bytes 1204232 | tf_op jit(solution)/shard_map/ppermute | solution.py:264
  46.7 10.9 %collective-permute-start.3 = (bf16[2,784,128]{2,1,0:T(8,128)(2,1)S(1)}, bf16[2,784,128]{2,1,0:T(8,128)(2,1)}, u32[]{:S(2)}, u32[]{:S(2)}) collective-permute-start(bf16[2,784,128]{2,1,0:T(8,128)(2,1)S(1)} %pad_maximum_fusion.1.refs_0_), channel_id=1, source_target_pairs={{0,2},{2,4},{4,6},{6,8},{8,10},{10,12},{12,14},{14,0},{1,3},{3,5},... | collective-permute-start | bytes 1204232 | tf_op jit(solution)/shard_map/ppermute | solution.py:263
  46.8 20.5 %collective-permute-start.13 = (bf16[2,1024,128]{2,1,0:T(8,128)(2,1)S(1)}, bf16[2,1024,128]{2,1,0:T(8,128)(2,1)}, u32[]{:S(2)}, u32[]{:S(2)}) collective-permute-start(bf16[2,1024,128]{2,1,0:T(8,128)(2,1)S(1)} %pad_maximum_fusion.refs_0_), channel_id=1, source_target_pairs={{0,32},{32,64},{64,96},{96,0},{1,33},{33,65},{65,97},{97,1},{2,34}... | collective-permute-start | bytes 1572872 | tf_op jit(solution)/shard_map/ppermute | solution.py:273
  50.1 18.8 %collective-permute-start.11 = (bf16[8,256,128]{2,1,0:T(8,128)(2,1)S(1)}, bf16[8,256,128]{2,1,0:T(8,128)(2,1)S(1)}, u32[]{:S(2)}, u32[]{:S(2)}) collective-permute-start(bf16[8,256,128]{2,1,0:T(8,128)(2,1)S(1)} %all-to-all-done.1.refs_4_.refs_3_.refs_5_), channel_id=1, source_target_pairs={{0,16},{16,0},{1,17},{17,1},{2,18},{18,2},{3,19},{19,3},{4,20},{20... | collective-permute-start | bytes 1572872 | tf_op jit(solution)/shard_map/ppermute | solution.py:260
  53.1 9.6 %collective-permute-start.7 = (bf16[2,784,128]{2,1,0:T(8,128)(2,1)S(1)}, bf16[2,784,128]{2,1,0:T(8,128)(2,1)S(1)}, u32[]{:S(2)}, u32[]{:S(2)}) collective-permute-start(bf16[2,784,128]{2,1,0:T(8,128)(2,1)S(1)} %collective-permute-done.6.refs_2_), channel_id=1, source_target_pairs={{0,14},{2,0},{4,2},{6,4},{8,6},{10,8},{12,10},{14,12},{1,15},{3,1}... | collective-permute-start | bytes 1204232 | tf_op jit(solution)/shard_map/ppermute | solution.py:264
  56.8 0.7 copy-start
  57.6 11.3 %collective-permute-start.4 = (bf16[2,784,128]{2,1,0:T(8,128)(2,1)}, bf16[2,784,128]{2,1,0:T(8,128)(2,1)S(1)}, u32[]{:S(2)}, u32[]{:S(2)}) collective-permute-start(bf16[2,784,128]{2,1,0:T(8,128)(2,1)} %collective-permute-done.3.refs_1_), channel_id=1, source_target_pairs={{0,2},{2,4},{4,6},{6,8},{8,10},{10,12},{12,14},{14,0},{1,3},{3,5},... | collective-permute-start | bytes 1204232 | tf_op jit(solution)/shard_map/ppermute | solution.py:263
  62.7 15.1 %collective-permute-start.8 = (bf16[2,784,128]{2,1,0:T(8,128)(2,1)S(1)}, bf16[2,784,128]{2,1,0:T(8,128)(2,1)S(1)}, u32[]{:S(2)}, u32[]{:S(2)}) collective-permute-start(bf16[2,784,128]{2,1,0:T(8,128)(2,1)S(1)} %collective-permute-done.7.refs_1_), channel_id=1, source_target_pairs={{0,14},{2,0},{4,2},{6,4},{8,6},{10,8},{12,10},{14,12},{1,15},{3,1}... | collective-permute-start | bytes 1204232 | tf_op jit(solution)/shard_map/ppermute | solution.py:264
  66.3 34.9 %collective-permute-start.16 = (bf16[2,1024,128]{2,1,0:T(8,128)(2,1)S(1)}, bf16[2,1024,128]{2,1,0:T(8,128)(2,1)S(1)}, u32[]{:S(2)}, u32[]{:S(2)}) collective-permute-start(bf16[2,1024,128]{2,1,0:T(8,128)(2,1)S(1)} %pad_maximum_fusion.refs_0_), channel_id=1, source_target_pairs={{0,128},{128,0},{1,129},{129,1},{2,130},{130,2},{3,131},{131,3},{4... | collective-permute-start | bytes 1572872 | tf_op jit(solution)/shard_map/ppermute | solution.py:272
  67.3 36.7 %collective-permute-start.14 = (bf16[2,1024,128]{2,1,0:T(8,128)(2,1)}, bf16[2,1024,128]{2,1,0:T(8,128)(2,1)S(1)}, u32[]{:S(2)}, u32[]{:S(2)}) collective-permute-start(bf16[2,1024,128]{2,1,0:T(8,128)(2,1)} %collective-permute-done.13.refs_1_), channel_id=1, source_target_pairs={{0,32},{32,64},{64,96},{96,0},{1,33},{33,65},{65,97},{97,1},{2,34}... | collective-permute-start | bytes 1572872 | tf_op jit(solution)/shard_map/ppermute | solution.py:275
  68.9 11.7 %collective-permute-start.5 = (bf16[2,784,128]{2,1,0:T(8,128)(2,1)S(1)}, bf16[2,784,128]{2,1,0:T(8,128)(2,1)S(1)}, u32[]{:S(2)}, u32[]{:S(2)}) collective-permute-start(bf16[2,784,128]{2,1,0:T(8,128)(2,1)S(1)} %collective-permute-done.4.refs_0_), channel_id=1, source_target_pairs={{0,2},{2,4},{4,6},{6,8},{8,10},{10,12},{12,14},{14,0},{1,3},{3,5},... | collective-permute-start | bytes 1204232 | tf_op jit(solution)/shard_map/ppermute | solution.py:263
  68.9 1.0 copy-start.1
  77.8 9.2 %collective-permute-start.10 = (bf16[784,128]{1,0:T(8,128)(2,1)S(1)}, bf16[784,128]{1,0:T(8,128)(2,1)S(1)}, u32[]{:S(2)}, u32[]{:S(2)}) collective-permute-start(bf16[784,128]{1,0:T(8,128)(2,1)S(1)} %slice_bitcast_fusion), channel_id=1, source_target_pairs={{0,14},{2,0},{4,2},{6,4},{8,6},{10,8},{12,10},{14,12},{1,15},{3,1}... | collective-permute-start | bytes 602120 | tf_op jit(solution)/shard_map/ppermute | solution.py:267
  80.6 6.4 %collective-permute-start.9 = (bf16[784,128]{1,0:T(8,128)(2,1)S(1)}, bf16[784,128]{1,0:T(8,128)(2,1)S(1)}, u32[]{:S(2)}, u32[]{:S(2)}) collective-permute-start(bf16[784,128]{1,0:T(8,128)(2,1)S(1)} %slice_bitcast_fusion.1), channel_id=1, source_target_pairs={{0,2},{2,4},{4,6},{6,8},{8,10},{10,12},{12,14},{14,0},{1,3},{3,5},... | collective-permute-start | bytes 602120 | tf_op jit(solution)/shard_map/ppermute | solution.py:266
  94.7 30.0 %collective-permute-start.12 = (bf16[512,1024]{1,0:T(8,128)(2,1)S(1)}, bf16[512,1024]{1,0:T(8,128)(2,1)S(1)}, u32[]{:S(2)}, u32[]{:S(2)}) collective-permute-start(bf16[512,1024]{1,0:T(8,128)(2,1)S(1)} %get-tuple-element.23), channel_id=1, source_target_pairs={{0,16},{16,0},{1,17},{17,1},{2,18},{18,2},{3,19},{19,3},{4,20},{20... | collective-permute-start | bytes 3145736 | tf_op jit(solution)/shard_map/ppermute | solution.py:282
  100.0 13.4 %collective-permute-start.15 = (bf16[2,1024,128]{2,1,0:T(8,128)(2,1)S(1)}, bf16[2,1024,128]{2,1,0:T(8,128)(2,1)S(1)}, u32[]{:S(2)}, u32[]{:S(2)}) collective-permute-start(bf16[2,1024,128]{2,1,0:T(8,128)(2,1)S(1)} %pad_maximum_fusion.refs_0_), channel_id=1, source_target_pairs={{0,96},{32,0},{64,32},{96,64},{1,97},{33,1},{65,33},{97,65},{2,98}... | collective-permute-start | bytes 1572872 | tf_op jit(solution)/shard_map/ppermute | solution.py:274
  101.2 14.3 %collective-permute-start.17 = (bf16[2,1024,128]{2,1,0:T(8,128)(2,1)S(1)}, bf16[2,1024,128]{2,1,0:T(8,128)(2,1)S(1)}, u32[]{:S(2)}, u32[]{:S(2)}) collective-permute-start(bf16[2,1024,128]{2,1,0:T(8,128)(2,1)S(1)} %collective-permute-done.16.refs_4_), channel_id=1, source_target_pairs={{0,32},{32,64},{64,96},{96,0},{1,33},{33,65},{65,97},{97,1},{2,34}... | collective-permute-start | bytes 1572872 | tf_op jit(solution)/shard_map/ppermute | solution.py:277
  101.5 23.2 %collective-permute-start.19 = (bf16[2,1024,128]{2,1,0:T(8,128)(2,1)S(1)}, bf16[2,1024,128]{2,1,0:T(8,128)(2,1)S(1)}, u32[]{:S(2)}, u32[]{:S(2)}) collective-permute-start(bf16[2,1024,128]{2,1,0:T(8,128)(2,1)S(1)} %collective-permute-done.16.refs_4_), channel_id=1, source_target_pairs={{0,96},{32,0},{64,32},{96,64},{1,97},{33,1},{65,33},{97,65},{2,98}... | collective-permute-start | bytes 1572872 | tf_op jit(solution)/shard_map/ppermute | solution.py:276
  103.9 20.7 %collective-permute-start.18 = (bf16[2,1024,128]{2,1,0:T(8,128)(2,1)S(1)}, bf16[2,1024,128]{2,1,0:T(8,128)(2,1)S(1)}, u32[]{:S(2)}, u32[]{:S(2)}) collective-permute-start(bf16[2,1024,128]{2,1,0:T(8,128)(2,1)S(1)} %collective-permute-done.14.refs_2_), channel_id=1, source_target_pairs={{0,128},{128,0},{1,129},{129,1},{2,130},{130,2},{3,131},{131,3},{4... | collective-permute-start | bytes 1572872 | tf_op jit(solution)/shard_map/ppermute | solution.py:278
  128.1 3.3 %collective-permute-start.20 = (bf16[8,512,128]{2,1,0:T(8,128)(2,1)S(1)}, bf16[8,512,128]{2,1,0:T(8,128)(2,1)S(1)}, u32[]{:S(2)}, u32[]{:S(2)}) collective-permute-start(bf16[8,512,128]{2,1,0:T(8,128)(2,1)S(1)} %get-tuple-element.26), channel_id=1, source_target_pairs={{0,16},{16,0},{1,17},{17,1},{2,18},{18,2},{3,19},{19,3},{4,20},{20... | collective-permute-start | bytes 3145736 | tf_op jit(solution)/shard_map/ppermute | solution.py:284

commit v3 on v2

--- a/solution.py
+++ b/solution.py
@@ -13,7 +13,8 @@
 F32 = jnp.float32
 BF16 = jnp.bfloat16
 PAY = 784
-LIMIT = pltpu.CompilerParams(vmem_limit_bytes=16 * 1024 * 1024)
+NEAR, MIDDLE, LAST = range(0, 6), range(6, 10), range(10, 16)
+LIMIT = pltpu.CompilerParams(vmem_limit_bytes=8 * 1024 * 1024)
 VM = pl.BlockSpec(memory_space=pltpu.VMEM)
 SM = pl.BlockSpec(memory_space=pltpu.SMEM)
 HB = pl.BlockSpec(memory_space=pltpu.HBM)
@@ -64,6 +65,27 @@
     )(*args)
 
 
+def fetch_kernel(pos, kern, rows, sems):
+    copies = [pltpu.make_async_copy(kern.at[pos[1 + n]], rows.at[n], sems.at[n]) for n in range(16)]
+    for copy in copies:
+        copy.start()
+    for copy in copies:
+        copy.wait()
+
+
+def fetch(pos, coulomb):
+    return pl.pallas_call(
+        fetch_kernel,
+        in_specs=[SM, HB],
+        out_specs=VM,
+        out_shape=jax.ShapeDtypeStruct((16, 128, 2048), BF16),
+        scratch_shapes=[pltpu.SemaphoreType.DMA((16,))],
+        compiler_params=LIMIT,
+        cost_estimate=cost(1 << 20, 8 << 20),
+        name="fetch",
+    )(pos, coulomb)
+
+
 def own_kernel(parts, out, spread):
     total = parts[0].astype(F32)
     for j in range(1, 8):
@@ -73,14 +95,14 @@
     for j in range(8):
         spread[j] = total[0:256]
     wide = total.astype(F32)
-    rows = []
+    sums = []
     for w in range(2):
         at = 256 * (w + 1)
         acc = jnp.sum(wide[0:128] * wide[at:at + 128].T, axis=0, keepdims=True)
         acc = acc + jnp.sum(wide[128:256] * wide[at + 128:at + 256].T, axis=0, keepdims=True)
-        rows.append(acc)
-    rows.append(jnp.zeros((14, 128), F32))
-    out[768:784] = jnp.concatenate(rows, axis=0).astype(BF16)
+        sums.append(acc)
+    sums.append(jnp.zeros((14, 128), F32))
+    out[768:784] = jnp.concatenate(sums, axis=0).astype(BF16)
 
 
 def own_points(parts):
@@ -95,30 +117,20 @@
     )(parts)
 
 
-def make_exchange_kernel(shapes, where, first, last):
+def make_exchange_kernel(shapes, which, first, last):
     def kernel(pos, *refs):
-        held = refs[:len(shapes)]
+        count = len(shapes)
+        held, (vals, same, cross), rest = refs[:count], refs[count:count + 3], refs[count + 3:]
         pays = []
         for ref, shape in zip(held, shapes):
             pays += [ref] if len(shape) == 2 else [ref.at[0], ref.at[1]]
-        kern, same, cross = refs[len(shapes):len(shapes) + 3]
-        rest = refs[len(shapes) + 3:]
-        if not first:
-            e_in, u_in = rest[:2]
-            rest = rest[2:]
-        v_buf, sems = rest[-2:]
-        rest = rest[:-2]
+        if first:
+            e_out, u_out = rest
+        elif last:
+            e_in, u_in, f_low, f_high = rest
+        else:
+            e_in, u_in, e_out, u_out = rest
         flag = pos[0] == 0
-
-        def fetch(h, b):
-            lanes = pl.ds(pl.multiple_of(512 * h, 512), 512)
-            return pltpu.make_async_copy(
-                kern.at[pos[1 + where[b]], :, lanes], v_buf.at[h, pl.ds(128 * b, 128)], sems.at[h, b]
-            )
-
-        for h in range(4):
-            for b in range(len(where)):
-                fetch(h, b).start()
 
         def theta(w):
             at = 256 * (w + 1)
@@ -126,27 +138,19 @@
                 [jnp.concatenate([p[at:at + 128], p[at + 128:at + 256]], axis=1) for p in pays], axis=0
             )
 
-        def pair_step(h, _):
-            for b in range(len(where)):
-                fetch(h, b).wait()
-            for half in range(2):
-                chip_step(h, half)
-            return 0
-
-        def chip_step(h, half):
-            chip = 2 * h + half
+        def chip_step(chip):
             xp = jnp.concatenate([p[0:256] for p in pays], axis=1)
             dens = jnp.concatenate([p[768:784] for p in pays], axis=1)
             lanes = pl.ds(pl.multiple_of(256 * chip, 256), 256)
             a = same[chip]
             b = cross[chip]
             xq = jnp.concatenate([jnp.where(flag, a, b), jnp.where(flag, b, a)], axis=1)
-            v = v_buf[h, :, 256 * half:256 * (half + 1)]
+            v = jnp.concatenate([vals[n, :, lanes] for n in which], axis=0)
             u = dot(dens, v, ((1,), (0,)))
             if not first:
                 u = u + u_in[:, lanes]
             if not last:
-                rest[1][:, lanes] = u
+                u_out[:, lanes] = u
             wide = v.astype(F32)
             for w in range(2):
                 tile = dot(theta(w), xq, ((1,), (0,)))
@@ -156,43 +160,43 @@
                 if not first:
                     e = e + e_in[rows, lanes]
                 if not last:
-                    rest[0][rows, lanes] = e
+                    e_out[rows, lanes] = e
                 else:
                     f = (u[w:w + 1] * xq.astype(F32) - e).astype(BF16)
                     here = pl.ds(pl.multiple_of(128 * chip, 128), 128)
                     low, high = f[:, 0:128], f[:, 128:256]
-                    rest[0][rows, here] = jnp.where(flag, low, high)
-                    rest[1][rows, here] = jnp.where(flag, high, low)
+                    f_low[rows, here] = jnp.where(flag, low, high)
+                    f_high[rows, here] = jnp.where(flag, high, low)
+
+        def pair_step(h, _):
+            chip_step(2 * h)
+            chip_step(2 * h + 1)
+            return 0
 
         lax.fori_loop(0, 4, pair_step, 0)
 
     return kernel
 
 
-def exchange(pos, held, where, coulomb, same, cross, totals, last):
+def exchange(pos, held, which, vals, same, cross, totals, last=False):
     first = totals is None
-    args = [pos, *held, coulomb, same, cross]
-    in_specs = [SM] + [VM] * len(held) + [HB, VM, VM]
+    args = [pos, *held, vals, same, cross]
     alias = {}
+    out_shape = [jax.ShapeDtypeStruct((512, 2048), F32), jax.ShapeDtypeStruct((16, 2048), F32)]
+    if last:
+        out_shape = [jax.ShapeDtypeStruct((512, 1024), BF16)] * 2
     if not first:
         if not last:
             alias = {len(args): 0, len(args) + 1: 1}
         args += list(totals)
-        in_specs += [VM, VM]
-    if last:
-        out_shape = [jax.ShapeDtypeStruct((512, 1024), BF16)] * 2
-    else:
-        out_shape = [jax.ShapeDtypeStruct((512, 2048), F32), jax.ShapeDtypeStruct((16, 2048), F32)]
-    rows = 128 * len(where)
-    return pl.pallas_call(
-        make_exchange_kernel([a.shape for a in held], where, first, last),
-        in_specs=in_specs,
+    return pl.pallas_call(
+        make_exchange_kernel([a.shape for a in held], which, first, last),
+        in_specs=[SM] + [VM] * (len(args) - 1),
         out_specs=[VM, VM],
         out_shape=out_shape,
-        scratch_shapes=[pltpu.VMEM((4, rows, 512), BF16), pltpu.SemaphoreType.DMA((4, len(where)))],
         input_output_aliases=alias,
         compiler_params=LIMIT,
-        cost_estimate=cost(8 * rows * 2048 * 256, 8 << 20),
+        cost_estimate=cost(1024 * len(which) * 2048 * 256, 8 << 20),
         name="exchange",
     )(*args)
 
@@ -276,9 +280,11 @@
     cols[7] = lax.ppermute(cols[4], "x", ring(4, -1))
     cols[5] = lax.ppermute(cols[4], "x", ring(4, 1))
     cols[6] = lax.ppermute(cols[2], "yl", swap())
-    totals = exchange(pos, [pair, up[1], down[1]], list(range(6)), coulomb, same, cross, None, False)
-    totals = exchange(pos, [up[2], down[2]], [6, 7, 8, 9], coulomb, same, cross, totals, False)
-    f_mine, f_give = exchange(pos, [up[3], down[3], *far], [10, 11, 12, 13, 14, 15], coulomb, same, cross, totals, True)
+    pos, _ = lax.optimization_barrier((pos, pair))
+    rows = fetch(pos, coulomb)
+    totals = exchange(pos, [pair, up[1], down[1]], NEAR, rows, same, cross, None)
+    totals = exchange(pos, [up[2], down[2]], MIDDLE, rows, same, cross, totals)
+    f_mine, f_give = exchange(pos, [up[3], down[3], *far], LAST, rows, same, cross, totals, True)
     f_got = lax.ppermute(f_give, "c", swap())
     keep, send = decode(pos, f_mine, f_got, cols)
     back = lax.ppermute(send, "c", swap())
@@ -300,4 +306,6 @@
 def solution(mesh):
     finer = Mesh(mesh.devices.reshape(2, 4, 2, 8, 2), ("yl", "x", "c", "z", "yh"))
     placed = (P(COL, ROW), P(None, None, ROW), P(None, ROW), P(None, ROW, COL))
-    return jax.shard_map(program, mesh=finer, in_specs=placed, out_specs=P(COL, None, ROW), check_vma=False)
+    return jax.shard_map(
+        program, mesh=finer, in_specs=placed, out_specs=P(COL, None, ROW), check_vma=False
+    )

time: 168 us -> 168 us (level)
    pallas_call x3 -> x4, Pallas kernels: 21.7 us -> 21.7 us  [the longest x3 17.6 us: exchange(): pl.pallas_call(make_exchange_kernel([a.shape for a in held], which, first...]
  transfers between devices with their start and end apart: 22 -> 22, of which waited for: 9 -> 10; matrix products, arithmetic and copies ran while one was open for 1% -> 1% of each run, Pallas kernels for 13% -> 13%
where the time goes in v3:
time: 168 us; the launch traced here: 167 us
  blocking collectives  58.9 us (35%)
  starting transfers between devices  40.7 us (24%)
  waiting for transfers between devices  35.9 us (21%)
  Pallas kernels  27.7 us (16%)
  local copies, waits for them, and re-layouts  2.55 us (2%)
    all_to_all x1, blocking collectives, program(): parts = lax.all_to_all(partial_value, CHIPS, 0, 0, tiled=True)  24.6 us
    all_to_all x1, blocking collectives, program(): terms = lax.all_to_all(both, CHIPS, 0, 0, tiled=True)  19.5 us
    pallas_call x3, Pallas kernels, exchange(): pl.pallas_call(make_exchange_kernel([a.shape for a in held], which, first...  17.6 us
    all_to_all x1, blocking collectives, program(): lax.all_to_all(summed.reshape(16, 32, 128), COL, 0, 0, tiled=True)  14.8 us
    ppermute x3, starting transfers between devices, program(): down.append(lax.ppermute(down[-1], 'z', ring(8, -1)))  12.9 us
    ppermute x1, waiting for transfers between devices, program(): cols[7] = lax.ppermute(cols[4], 'x', ring(4, -1))  9.07 us
    ppermute x1, waiting for transfers between devices, program(): cols[3] = lax.ppermute(base, 'x', ring(4, -1))  8.59 us
    ppermute x3, waiting for transfers between devices, program(): down.append(lax.ppermute(down[-1], 'z', ring(8, -1)))  7.33 us
  transfers between devices with their start and end apart: 22, of which 10 were waited for; matrix products, arithmetic and copies ran while one was open for 1% of the time, Pallas kernels for 13%

profile of v3, /device:TPU:1, one launch (start us, length us, event | category | flops | bytes accessed | tf_op | source)
XLA Modules:
  0.0 167.2 jit_solution(54894980473384281)
XLA Ops:
  0.0 1.1 dynamic-slice_bitcast_fusion
  1.1 3.3 %collective-permute-start = (bf16[8,128,128]{2,1,0:T(8,128)(2,1)S(1)}, bf16[8,128,128]{2,1,0:T(8,128)(2,1)S(1)}, u32[]{:S(2)}, u32[]{:S(2)}) collective-permute-start(bf16[8,128,128]{2,1,0:T(8,128)(2,1)S(1)} %get-tuple-element.29), channel_id=1, source_target_pairs={{0,16},{16,0},{1,17},{17,1},{2,18},{18,2},{3,19},{19,3},{4,20},{20... | collective-permute-start | bytes 786440 | tf_op jit(solution)/shard_map/ppermute | solution.py:255
  4.4 0.9 pad_maximum_fusion.2.stacked
  5.3 0.1 collective-permute-start.1
  5.4 1.4 collective-permute-done.1.other
  6.8 0.0 collective-permute-done.got
  6.8 1.3 encode.1
  8.1 24.6 %all_to_all.20.parts = bf16[8,256,384]{2,1,0:T(8,128)(2,1)S(1)} all-to-all(bf16[8,256,384]{2,1,0:T(8,128)(2,1)S(1)} %encode.1), channel_id=1, replica_groups=mesh['yl'=2,'x'=4,'c'=2,'z'=8,'yh'=2] {'yl','x'}, dimensions={0} | all-to-all | bytes 3145728 | tf_op jit(solution)/shard_map/all_to_all | solution.py:258
  32.7 1.0 own.1
  33.8 2.6 %collective-permute-start.2 = (bf16[784,128]{1,0:T(8,128)(2,1)S(1)}, bf16[784,128]{1,0:T(8,128)(2,1)S(1)}, u32[]{:S(2)}, u32[]{:S(2)}) collective-permute-start(bf16[784,128]{1,0:T(8,128)(2,1)S(1)} %get-tuple-element.17), channel_id=1, source_target_pairs={{0,1},{1,0},{2,3},{3,2},{4,5},{5,4},{6,7},{7,6},{8,9},{9,8},{10,11... | collective-permute-start | bytes 602120 | tf_op jit(solution)/shard_map/ppermute | solution.py:261
  36.4 3.5 %all-to-all-start.1 = ((bf16[8,256,128]{2,1,0:T(8,128)(2,1)}), bf16[8,256,128]{2,1,0:T(8,128)(2,1)S(1)}, u32[]{:S(2)}, u32[]{:S(2)}) async-start(bf16[8,256,128]{2,1,0:T(8,128)(2,1)} %get-tuple-element.19), calls=%async_computation.1 | async-start | bytes 1048576 | tf_op jit(solution)/shard_map/all_to_all | solution.py:263
  39.9 1.1 collective-permute-done.2
  41.1 5.7 %collective-permute-start.6 = (bf16[2,784,128]{2,1,0:T(8,128)(2,1)S(1)}, bf16[2,784,128]{2,1,0:T(8,128)(2,1)S(1)}, u32[]{:S(2)}, u32[]{:S(2)}) collective-permute-start(bf16[2,784,128]{2,1,0:T(8,128)(2,1)S(1)} %pad_maximum_fusion.1.refs_0_), channel_id=1, source_target_pairs={{0,14},{2,0},{4,2},{6,4},{8,6},{10,8},{12,10},{14,12},{1,15},{3,1}... | collective-permute-start | bytes 1204232 | tf_op jit(solution)/shard_map/ppermute | solution.py:268
  46.7 0.1 pad_maximum_fusion.refs_0_
  46.8 0.3 collective-permute-start.13
  47.1 3.0 %all-to-all-done.1.refs_4_.refs_3_.refs_5_ = bf16[8,256,128]{2,1,0:T(8,128)(2,1)S(1)} async-done(((bf16[8,256,128]{2,1,0:T(8,128)(2,1)}), bf16[8,256,128]{2,1,0:T(8,128)(2,1)S(1)}, u32[]{:S(2)}, u32[]{:S(2)}) %all-to-all-start.1) | async-done | bytes 524320 | tf_op jit(solution)/shard_map/all_to_all | solution.py:263
  50.1 0.8 collective-permute-start.11
  50.9 2.2 %collective-permute-done.6.refs_2_ = bf16[2,784,128]{2,1,0:T(8,128)(2,1)S(1)} collective-permute-done((bf16[2,784,128]{2,1,0:T(8,128)(2,1)S(1)}, bf16[2,784,128]{2,1,0:T(8,128)(2,1)S(1)}, u32[]{:S(2)}, u32[]{:S(2)}) %collective-permute-start.6) | collective-permute-done | bytes 401440 | tf_op jit(solution)/shard_map/ppermute | solution.py:268
  53.1 3.7 %collective-permute-start.7 = (bf16[2,784,128]{2,1,0:T(8,128)(2,1)S(1)}, bf16[2,784,128]{2,1,0:T(8,128)(2,1)S(1)}, u32[]{:S(2)}, u32[]{:S(2)}) collective-permute-start(bf16[2,784,128]{2,1,0:T(8,128)(2,1)S(1)} %collective-permute-done.6.refs_2_), channel_id=1, source_target_pairs={{0,14},{2,0},{4,2},{6,4},{8,6},{10,8},{12,10},{14,12},{1,15},{3,1}... | collective-permute-start | bytes 1204232 | tf_op jit(solution)/shard_map/ppermute | solution.py:268
  56.8 0.7 copy-done
  57.6 5.1 %collective-permute-done.7.refs_1_ = bf16[2,784,128]{2,1,0:T(8,128)(2,1)S(1)} collective-permute-done((bf16[2,784,128]{2,1,0:T(8,128)(2,1)S(1)}, bf16[2,784,128]{2,1,0:T(8,128)(2,1)S(1)}, u32[]{:S(2)}, u32[]{:S(2)}) %collective-permute-start.7) | collective-permute-done | bytes 401440 | tf_op jit(solution)/shard_map/ppermute | solution.py:268
  62.7 3.5 %collective-permute-start.8 = (bf16[2,784,128]{2,1,0:T(8,128)(2,1)S(1)}, bf16[2,784,128]{2,1,0:T(8,128)(2,1)S(1)}, u32[]{:S(2)}, u32[]{:S(2)}) collective-permute-start(bf16[2,784,128]{2,1,0:T(8,128)(2,1)S(1)} %collective-permute-done.7.refs_1_), channel_id=1, source_target_pairs={{0,14},{2,0},{4,2},{6,4},{8,6},{10,8},{12,10},{14,12},{1,15},{3,1}... | collective-permute-start | bytes 1204232 | tf_op jit(solution)/shard_map/ppermute | solution.py:268
  66.2 0.1 stack.91.pos
  66.3 1.0 collective-permute-start.16
  67.3 4.1 %fetch.1.refs_3_.refs_2_.refs_4_ = bf16[16,128,2048]{2,1,0:T(8,128)(2,1)S(1)} custom-call(s32[19]{0:T(128)S(1)} %stack.91.pos, bf16[16,128,2048]{2,1,0:T(8,128)(2,1)} %kern.1), custom_call_target="tpu_custom_call" | custom-call | flops 1048576 | bytes 8388608 | tf_op jit(solution)/shard_map/fetch/pallas_call | solution.py:77
  71.3 1.7 %collective-permute-start.14 = (bf16[2,1024,128]{2,1,0:T(8,128)(2,1)}, bf16[2,1024,128]{2,1,0:T(8,128)(2,1)S(1)}, u32[]{:S(2)}, u32[]{:S(2)}) collective-permute-start(bf16[2,1024,128]{2,1,0:T(8,128)(2,1)} %collective-permute-done.13.refs_1_), channel_id=1, source_target_pairs={{0,32},{32,64},{64,96},{96,0},{1,33},{33,65},{65,97},{97,1},{2,34}... | collective-permute-start | bytes 1572872 | tf_op jit(solution)/shard_map/ppermute | solution.py:279
  73.1 6.5 %exchange.3 = (f32[512,2048]{1,0:T(8,128)S(1)}, f32[16,2048]{1,0:T(8,128)S(1)}) custom-call(s32[19]{0:T(128)S(1)} %stack.91.pos, bf16[2,784,128]{2,1,0:T(8,128)(2,1)S(1)} %pad_maximum_fusion.1.refs_0_, bf16[2,784,128]{2,1,0:T(8,128)(2,1)} %collective-permute-done.3.refs_1_, bf16[2,784,128]{2,1,0:T(8,128)(2,1)S(1)} %copy-done.1, ...), custom_call_target="tpu_custom_call" | custom-call | flops 3221225472 | bytes 8388608 | tf_op jit(solution)/shard_map/exchange/pallas_call | solution.py:192
  79.6 2.7 %collective-permute-start.10 = (bf16[784,128]{1,0:T(8,128)(2,1)S(1)}, bf16[784,128]{1,0:T(8,128)(2,1)S(1)}, u32[]{:S(2)}, u32[]{:S(2)}) collective-permute-start(bf16[784,128]{1,0:T(8,128)(2,1)S(1)} %slice_bitcast_fusion), channel_id=1, source_target_pairs={{0,14},{2,0},{4,2},{6,4},{8,6},{10,8},{12,10},{14,12},{1,15},{3,1}... | collective-permute-start | bytes 602120 | tf_op jit(solution)/shard_map/ppermute | solution.py:271
  82.3 0.3 collective-permute-start.9
  82.6 4.9 %exchange.4 = (f32[512,2048]{1,0:T(8,128)S(1)}, f32[16,2048]{1,0:T(8,128)S(1)}) custom-call(s32[19]{0:T(128)S(1)} %stack.91.pos, bf16[2,784,128]{2,1,0:T(8,128)(2,1)S(1)} %collective-permute-done.4.refs_0_, bf16[2,784,128]{2,1,0:T(8,128)(2,1)S(1)} %collective-permute-done.7.refs_1_, ...), custom_call_target="tpu_custom_call", output_to_operand_aliasing={{0}: (6, {}), {1}: (7, {})} | custom-call | flops 2147483648 | bytes 8388608 | tf_op jit(solution)/shard_map/exchange/pallas_call | solution.py:192
  87.5 0.8 collective-permute-done.9.refs_2_
  88.3 6.2 %exchange.5 = (bf16[512,1024]{1,0:T(8,128)(2,1)S(1)}, bf16[512,1024]{1,0:T(8,128)(2,1)S(1)}) custom-call(s32[19]{0:T(128)S(1)} %stack.91.pos, bf16[2,784,128]{2,1,0:T(8,128)(2,1)S(1)} %collective-permute-done.5.refs_0_, bf16[2,784,128]{2,1,0:T(8,128)(2,1)S(1)} %collective-permute-done.8.refs_1_, bf16[784,128]{1,0:T(8,128)(2,1)S(1)} %collective-permute-done.9.refs_2_, ...), custom_call_target="tpu_custom_call" | custom-call | flops 3221225472 | bytes 8388608 | tf_op jit(solution)/shard_map/exchange/pallas_call | solution.py:192
  94.6 5.7 %collective-permute-start.12 = (bf16[512,1024]{1,0:T(8,128)(2,1)S(1)}, bf16[512,1024]{1,0:T(8,128)(2,1)S(1)}, u32[]{:S(2)}, u32[]{:S(2)}) collective-permute-start(bf16[512,1024]{1,0:T(8,128)(2,1)S(1)} %get-tuple-element.25), channel_id=1, source_target_pairs={{0,16},{16,0},{1,17},{17,1},{2,18},{18,2},{3,19},{19,3},{4,20},{20... | collective-permute-start | bytes 3145736 | tf_op jit(solution)/shard_map/ppermute | solution.py:288
  100.3 1.2 collective-permute-start.15
  101.6 0.2 collective-permute-start.17
  101.8 2.4 %collective-permute-start.19 = (bf16[2,1024,128]{2,1,0:T(8,128)(2,1)S(1)}, bf16[2,1024,128]{2,1,0:T(8,128)(2,1)S(1)}, u32[]{:S(2)}, u32[]{:S(2)}) collective-permute-start(bf16[2,1024,128]{2,1,0:T(8,128)(2,1)S(1)} %collective-permute-done.16.refs_4_), channel_id=1, source_target_pairs={{0,96},{32,0},{64,32},{96,64},{1,97},{33,1},{65,33},{97,65},{2,98}... | collective-permute-start | bytes 1572872 | tf_op jit(solution)/shard_map/ppermute | solution.py:280
  104.2 0.9 collective-permute-start.18
  105.1 8.6 %collective-permute-done.15.refs_3_ = bf16[2,1024,128]{2,1,0:T(8,128)(2,1)S(1)} collective-permute-done((bf16[2,1024,128]{2,1,0:T(8,128)(2,1)S(1)}, bf16[2,1024,128]{2,1,0:T(8,128)(2,1)S(1)}, u32[]{:S(2)}, u32[]{:S(2)}) %collective-permute-start.15) | collective-permute-done | bytes 524320 | tf_op jit(solution)/shard_map/ppermute | solution.py:278
  113.7 2.2 %collective-permute-done.17.refs_5_ = bf16[2,1024,128]{2,1,0:T(8,128)(2,1)S(1)} collective-permute-done((bf16[2,1024,128]{2,1,0:T(8,128)(2,1)S(1)}, bf16[2,1024,128]{2,1,0:T(8,128)(2,1)S(1)}, u32[]{:S(2)}, u32[]{:S(2)}) %collective-permute-start.17) | collective-permute-done | bytes 524320 | tf_op jit(solution)/shard_map/ppermute | solution.py:281
  115.9 9.1 %collective-permute-done.19.refs_7_ = bf16[2,1024,128]{2,1,0:T(8,128)(2,1)S(1)} collective-permute-done((bf16[2,1024,128]{2,1,0:T(8,128)(2,1)S(1)}, bf16[2,1024,128]{2,1,0:T(8,128)(2,1)S(1)}, u32[]{:S(2)}, u32[]{:S(2)}) %collective-permute-start.19) | collective-permute-done | bytes 524320 | tf_op jit(solution)/shard_map/ppermute | solution.py:280
  125.0 3.5 %decode.1 = (bf16[8,512,128]{2,1,0:T(8,128)(2,1)S(1)}, bf16[8,512,128]{2,1,0:T(8,128)(2,1)S(1)}) custom-call(s32[19]{0:T(128)S(1)} %stack.91.pos, bf16[512,1024]{1,0:T(8,128)(2,1)S(1)} %get-tuple-element.24.f_mine, bf16[512,1024]{1,0:T(8,128)(2,1)S(1)} %collective-permute-done.12.f_got, bf16[2,1024,128]{2,1,0:T(8,128)(2,1)S(1)} %pad_maximum_fusion.refs_0_, ...), custom_call_target="tpu_custom_call" | custom-call | flops 2147483648 | bytes 8388608 | tf_op jit(solution)/shard_map/decode/pallas_call | solution.py:216
  128.5 1.0 collective-permute-start.20
  129.5 2.3 %collective-permute-done.20 = bf16[8,512,128]{2,1,0:T(8,128)(2,1)S(1)} collective-permute-done((bf16[8,512,128]{2,1,0:T(8,128)(2,1)S(1)}, bf16[8,512,128]{2,1,0:T(8,128)(2,1)S(1)}, u32[]{:S(2)}, u32[]{:S(2)}) %collective-permute-start.20) | collective-permute-done | bytes 1048608 | tf_op jit(solution)/shard_map/ppermute | solution.py:290
  131.8 0.3 add_convert_fusion
  132.1 19.5 %all_to_all.21.parts = bf16[8,512,128]{2,1,0:T(8,128)(2,1)S(1)} all-to-all(bf16[8,512,128]{2,1,0:T(8,128)(2,1)S(1)} %add_convert_fusion), channel_id=1, replica_groups=mesh['yl'=2,'x'=4,'c'=2,'z'=8,'yh'=2] {'yl','x'}, dimensions={0} | all-to-all | bytes 2097152 | tf_op jit(solution)/shard_map/all_to_all | solution.py:292
  151.6 0.1 chip_sum.1
  151.7 14.8 %all_to_all.22 = bf16[16,32,128]{2,1,0:T(8,128)(2,1)S(1)} all-to-all(bf16[16,32,128]{2,1,0:T(8,128)(2,1)S(1)} %bitcast.44), channel_id=1, replica_groups=mesh['yl'=2,'x'=4,'c'=2,'z'=8,'yh'=2] {'z','yh'}, dimensions={0} | all-to-all | bytes 262144 | tf_op jit(solution)/shard_map/all_to_all | solution.py:301
  166.6 0.6 copy.11
  (22 shorter events, 0.1 us)
Async XLA Ops:
  1.1 5.7 %collective-permute-start = (bf16[8,128,128]{2,1,0:T(8,128)(2,1)S(1)}, bf16[8,128,128]{2,1,0:T(8,128)(2,1)S(1)}, u32[]{:S(2)}, u32[]{:S(2)}) collective-permute-start(bf16[8,128,128]{2,1,0:T(8,128)(2,1)S(1)} %get-tuple-element.29), channel_id=1, source_target_pairs={{0,16},{16,0},{1,17},{17,1},{2,18},{18,2},{3,19},{19,3},{4,20},{20... | collective-permute-start | bytes 786440 | tf_op jit(solution)/shard_map/ppermute | solution.py:255
  5.3 1.5 collective-permute-start.1
  33.8 7.2 %collective-permute-start.2 = (bf16[784,128]{1,0:T(8,128)(2,1)S(1)}, bf16[784,128]{1,0:T(8,128)(2,1)S(1)}, u32[]{:S(2)}, u32[]{:S(2)}) collective-permute-start(bf16[784,128]{1,0:T(8,128)(2,1)S(1)} %get-tuple-element.17), channel_id=1, source_target_pairs={{0,1},{1,0},{2,3},{3,2},{4,5},{5,4},{6,7},{7,6},{8,9},{9,8},{10,11... | collective-permute-start | bytes 602120 | tf_op jit(solution)/shard_map/ppermute | solution.py:261
  36.4 13.7 %all-to-all-start.1 = ((bf16[8,256,128]{2,1,0:T(8,128)(2,1)}), bf16[8,256,128]{2,1,0:T(8,128)(2,1)S(1)}, u32[]{:S(2)}, u32[]{:S(2)}) async-start(bf16[8,256,128]{2,1,0:T(8,128)(2,1)} %get-tuple-element.19), calls=%async_computation.1 | async-start | bytes 1048576 | tf_op jit(solution)/shard_map/all_to_all | solution.py:263
  41.1 12.0 %collective-permute-start.6 = (bf16[2,784,128]{2,1,0:T(8,128)(2,1)S(1)}, bf16[2,784,128]{2,1,0:T(8,128)(2,1)S(1)}, u32[]{:S(2)}, u32[]{:S(2)}) collective-permute-start(bf16[2,784,128]{2,1,0:T(8,128)(2,1)S(1)} %pad_maximum_fusion.1.refs_0_), channel_id=1, source_target_pairs={{0,14},{2,0},{4,2},{6,4},{8,6},{10,8},{12,10},{14,12},{1,15},{3,1}... | collective-permute-start | bytes 1204232 | tf_op jit(solution)/shard_map/ppermute | solution.py:268
  46.7 10.9 %collective-permute-start.3 = (bf16[2,784,128]{2,1,0:T(8,128)(2,1)S(1)}, bf16[2,784,128]{2,1,0:T(8,128)(2,1)}, u32[]{:S(2)}, u32[]{:S(2)}) collective-permute-start(bf16[2,784,128]{2,1,0:T(8,128)(2,1)S(1)} %pad_maximum_fusion.1.refs_0_), channel_id=1, source_target_pairs={{0,2},{2,4},{4,6},{6,8},{8,10},{10,12},{12,14},{14,0},{1,3},{3,5},... | collective-permute-start | bytes 1204232 | tf_op jit(solution)/shard_map/ppermute | solution.py:267
  46.8 24.6 %collective-permute-start.13 = (bf16[2,1024,128]{2,1,0:T(8,128)(2,1)S(1)}, bf16[2,1024,128]{2,1,0:T(8,128)(2,1)}, u32[]{:S(2)}, u32[]{:S(2)}) collective-permute-start(bf16[2,1024,128]{2,1,0:T(8,128)(2,1)S(1)} %pad_maximum_fusion.refs_0_), channel_id=1, source_target_pairs={{0,32},{32,64},{64,96},{96,0},{1,33},{33,65},{65,97},{97,1},{2,34}... | collective-permute-start | bytes 1572872 | tf_op jit(solution)/shard_map/ppermute | solution.py:277
  50.1 23.0 %collective-permute-start.11 = (bf16[8,256,128]{2,1,0:T(8,128)(2,1)S(1)}, bf16[8,256,128]{2,1,0:T(8,128)(2,1)S(1)}, u32[]{:S(2)}, u32[]{:S(2)}) collective-permute-start(bf16[8,256,128]{2,1,0:T(8,128)(2,1)S(1)} %all-to-all-done.1.refs_4_.refs_3_.refs_5_), channel_id=1, source_target_pairs={{0,16},{16,0},{1,17},{17,1},{2,18},{18,2},{3,19},{19,3},{4,20},{20... | collective-permute-start | bytes 1572872 | tf_op jit(solution)/shard_map/ppermute | solution.py:264
  53.1 9.6 %collective-permute-start.7 = (bf16[2,784,128]{2,1,0:T(8,128)(2,1)S(1)}, bf16[2,784,128]{2,1,0:T(8,128)(2,1)S(1)}, u32[]{:S(2)}, u32[]{:S(2)}) collective-permute-start(bf16[2,784,128]{2,1,0:T(8,128)(2,1)S(1)} %collective-permute-done.6.refs_2_), channel_id=1, source_target_pairs={{0,14},{2,0},{4,2},{6,4},{8,6},{10,8},{12,10},{14,12},{1,15},{3,1}... | collective-permute-start | bytes 1204232 | tf_op jit(solution)/shard_map/ppermute | solution.py:268
  56.8 0.7 copy-start
  57.6 15.5 %collective-permute-start.4 = (bf16[2,784,128]{2,1,0:T(8,128)(2,1)}, bf16[2,784,128]{2,1,0:T(8,128)(2,1)S(1)}, u32[]{:S(2)}, u32[]{:S(2)}) collective-permute-start(bf16[2,784,128]{2,1,0:T(8,128)(2,1)} %collective-permute-done.3.refs_1_), channel_id=1, source_target_pairs={{0,2},{2,4},{4,6},{6,8},{8,10},{10,12},{12,14},{14,0},{1,3},{3,5},... | collective-permute-start | bytes 1204232 | tf_op jit(solution)/shard_map/ppermute | solution.py:267
  62.7 16.9 %collective-permute-start.8 = (bf16[2,784,128]{2,1,0:T(8,128)(2,1)S(1)}, bf16[2,784,128]{2,1,0:T(8,128)(2,1)S(1)}, u32[]{:S(2)}, u32[]{:S(2)}) collective-permute-start(bf16[2,784,128]{2,1,0:T(8,128)(2,1)S(1)} %collective-permute-done.7.refs_1_), channel_id=1, source_target_pairs={{0,14},{2,0},{4,2},{6,4},{8,6},{10,8},{12,10},{14,12},{1,15},{3,1}... | collective-permute-start | bytes 1204232 | tf_op jit(solution)/shard_map/ppermute | solution.py:268
  66.3 6.8 %copy-start.1 = (bf16[2,784,128]{2,1,0:T(8,128)(2,1)S(1)}, bf16[2,784,128]{2,1,0:T(8,128)(2,1)}, u32[]{:S(2)}) copy-start(bf16[2,784,128]{2,1,0:T(8,128)(2,1)} %copy-done) | copy-start | bytes 1204228
  66.3 35.3 %collective-permute-start.16 = (bf16[2,1024,128]{2,1,0:T(8,128)(2,1)S(1)}, bf16[2,1024,128]{2,1,0:T(8,128)(2,1)S(1)}, u32[]{:S(2)}, u32[]{:S(2)}) collective-permute-start(bf16[2,1024,128]{2,1,0:T(8,128)(2,1)S(1)} %pad_maximum_fusion.refs_0_), channel_id=1, source_target_pairs={{0,128},{128,0},{1,129},{129,1},{2,130},{130,2},{3,131},{131,3},{4... | collective-permute-start | bytes 1572872 | tf_op jit(solution)/shard_map/ppermute | solution.py:276
  71.3 32.9 %collective-permute-start.14 = (bf16[2,1024,128]{2,1,0:T(8,128)(2,1)}, bf16[2,1024,128]{2,1,0:T(8,128)(2,1)S(1)}, u32[]{:S(2)}, u32[]{:S(2)}) collective-permute-start(bf16[2,1024,128]{2,1,0:T(8,128)(2,1)} %collective-permute-done.13.refs_1_), channel_id=1, source_target_pairs={{0,32},{32,64},{64,96},{96,0},{1,33},{33,65},{65,97},{97,1},{2,34}... | collective-permute-start | bytes 1572872 | tf_op jit(solution)/shard_map/ppermute | solution.py:279
  73.0 9.3 %collective-permute-start.5 = (bf16[2,784,128]{2,1,0:T(8,128)(2,1)S(1)}, bf16[2,784,128]{2,1,0:T(8,128)(2,1)S(1)}, u32[]{:S(2)}, u32[]{:S(2)}) collective-permute-start(bf16[2,784,128]{2,1,0:T(8,128)(2,1)S(1)} %collective-permute-done.4.refs_0_), channel_id=1, source_target_pairs={{0,2},{2,4},{4,6},{6,8},{8,10},{10,12},{12,14},{14,0},{1,3},{3,5},... | collective-permute-start | bytes 1204232 | tf_op jit(solution)/shard_map/ppermute | solution.py:267
  79.6 7.9 %collective-permute-start.10 = (bf16[784,128]{1,0:T(8,128)(2,1)S(1)}, bf16[784,128]{1,0:T(8,128)(2,1)S(1)}, u32[]{:S(2)}, u32[]{:S(2)}) collective-permute-start(bf16[784,128]{1,0:T(8,128)(2,1)S(1)} %slice_bitcast_fusion), channel_id=1, source_target_pairs={{0,14},{2,0},{4,2},{6,4},{8,6},{10,8},{12,10},{14,12},{1,15},{3,1}... | collective-permute-start | bytes 602120 | tf_op jit(solution)/shard_map/ppermute | solution.py:271
  82.3 6.0 %collective-permute-start.9 = (bf16[784,128]{1,0:T(8,128)(2,1)S(1)}, bf16[784,128]{1,0:T(8,128)(2,1)S(1)}, u32[]{:S(2)}, u32[]{:S(2)}) collective-permute-start(bf16[784,128]{1,0:T(8,128)(2,1)S(1)} %slice_bitcast_fusion.1), channel_id=1, source_target_pairs={{0,2},{2,4},{4,6},{6,8},{8,10},{10,12},{12,14},{14,0},{1,3},{3,5},... | collective-permute-start | bytes 602120 | tf_op jit(solution)/shard_map/ppermute | solution.py:270
  94.6 30.3 %collective-permute-start.12 = (bf16[512,1024]{1,0:T(8,128)(2,1)S(1)}, bf16[512,1024]{1,0:T(8,128)(2,1)S(1)}, u32[]{:S(2)}, u32[]{:S(2)}) collective-permute-start(bf16[512,1024]{1,0:T(8,128)(2,1)S(1)} %get-tuple-element.25), channel_id=1, source_target_pairs={{0,16},{16,0},{1,17},{17,1},{2,18},{18,2},{3,19},{19,3},{4,20},{20... | collective-permute-start | bytes 3145736 | tf_op jit(solution)/shard_map/ppermute | solution.py:288
  100.3 13.4 %collective-permute-start.15 = (bf16[2,1024,128]{2,1,0:T(8,128)(2,1)S(1)}, bf16[2,1024,128]{2,1,0:T(8,128)(2,1)S(1)}, u32[]{:S(2)}, u32[]{:S(2)}) collective-permute-start(bf16[2,1024,128]{2,1,0:T(8,128)(2,1)S(1)} %pad_maximum_fusion.refs_0_), channel_id=1, source_target_pairs={{0,96},{32,0},{64,32},{96,64},{1,97},{33,1},{65,33},{97,65},{2,98}... | collective-permute-start | bytes 1572872 | tf_op jit(solution)/shard_map/ppermute | solution.py:278
  101.6 14.3 %collective-permute-start.17 = (bf16[2,1024,128]{2,1,0:T(8,128)(2,1)S(1)}, bf16[2,1024,128]{2,1,0:T(8,128)(2,1)S(1)}, u32[]{:S(2)}, u32[]{:S(2)}) collective-permute-start(bf16[2,1024,128]{2,1,0:T(8,128)(2,1)S(1)} %collective-permute-done.16.refs_4_), channel_id=1, source_target_pairs={{0,32},{32,64},{64,96},{96,0},{1,33},{33,65},{65,97},{97,1},{2,34}... | collective-permute-start | bytes 1572872 | tf_op jit(solution)/shard_map/ppermute | solution.py:281
  101.8 23.2 %collective-permute-start.19 = (bf16[2,1024,128]{2,1,0:T(8,128)(2,1)S(1)}, bf16[2,1024,128]{2,1,0:T(8,128)(2,1)S(1)}, u32[]{:S(2)}, u32[]{:S(2)}) collective-permute-start(bf16[2,1024,128]{2,1,0:T(8,128)(2,1)S(1)} %collective-permute-done.16.refs_4_), channel_id=1, source_target_pairs={{0,96},{32,0},{64,32},{96,64},{1,97},{33,1},{65,33},{97,65},{2,98}... | collective-permute-start | bytes 1572872 | tf_op jit(solution)/shard_map/ppermute | solution.py:280
  104.2 20.7 %collective-permute-start.18 = (bf16[2,1024,128]{2,1,0:T(8,128)(2,1)S(1)}, bf16[2,1024,128]{2,1,0:T(8,128)(2,1)S(1)}, u32[]{:S(2)}, u32[]{:S(2)}) collective-permute-start(bf16[2,1024,128]{2,1,0:T(8,128)(2,1)S(1)} %collective-permute-done.14.refs_2_), channel_id=1, source_target_pairs={{0,128},{128,0},{1,129},{129,1},{2,130},{130,2},{3,131},{131,3},{4... | collective-permute-start | bytes 1572872 | tf_op jit(solution)/shard_map/ppermute | solution.py:282
  128.5 3.3 %collective-permute-start.20 = (bf16[8,512,128]{2,1,0:T(8,128)(2,1)S(1)}, bf16[8,512,128]{2,1,0:T(8,128)(2,1)S(1)}, u32[]{:S(2)}, u32[]{:S(2)}) collective-permute-start(bf16[8,512,128]{2,1,0:T(8,128)(2,1)S(1)} %get-tuple-element.28), channel_id=1, source_target_pairs={{0,16},{16,0},{1,17},{17,1},{2,18},{18,2},{3,19},{19,3},{4,20},{20... | collective-permute-start | bytes 3145736 | tf_op jit(solution)/shard_map/ppermute | solution.py:290

commit v4 on v3

--- a/solution.py
+++ b/solution.py
@@ -13,7 +13,7 @@
 F32 = jnp.float32
 BF16 = jnp.bfloat16
 PAY = 784
-NEAR, MIDDLE, LAST = range(0, 6), range(6, 10), range(10, 16)
+NEAR, MIDDLE, OUTER, LAST = range(0, 6), range(6, 10), range(10, 14), range(14, 16)
 LIMIT = pltpu.CompilerParams(vmem_limit_bytes=8 * 1024 * 1024)
 VM = pl.BlockSpec(memory_space=pltpu.VMEM)
 SM = pl.BlockSpec(memory_space=pltpu.SMEM)
@@ -284,7 +284,8 @@
     rows = fetch(pos, coulomb)
     totals = exchange(pos, [pair, up[1], down[1]], NEAR, rows, same, cross, None)
     totals = exchange(pos, [up[2], down[2]], MIDDLE, rows, same, cross, totals)
-    f_mine, f_give = exchange(pos, [up[3], down[3], *far], LAST, rows, same, cross, totals, True)
+    totals = exchange(pos, [up[3], down[3]], OUTER, rows, same, cross, totals)
+    f_mine, f_give = exchange(pos, far, LAST, rows, same, cross, totals, True)
     f_got = lax.ppermute(f_give, "c", swap())
     keep, send = decode(pos, f_mine, f_got, cols)
     back = lax.ppermute(send, "c", swap())

time: 168 us -> 174 us (1.036)
  waiting for transfers between devices: 35.9 us -> 39.9 us
  Pallas kernels: 27.7 us -> 29.7 us
    ppermute x3, waiting for transfers between devices: 0.01 us -> 12.4 us  [program(): up.append(lax.ppermute(up[-1], 'z', ring(8, 1)))]
    ppermute x3, waiting for transfers between devices: 7.33 us -> 0.22 us  [program(): down.append(lax.ppermute(down[-1], 'z', ring(8, -1)))]
    pallas_call x3 -> x4, Pallas kernels: 17.6 us -> 20.2 us  [exchange(): pl.pallas_call(make_exchange_kernel([a.shape for a in held], which, first...]
    ppermute x3, starting transfers between devices: 0.01 us -> 2.29 us  [program(): up.append(lax.ppermute(up[-1], 'z', ring(8, 1)))]
    ppermute x1, starting transfers between devices: 5.72 us -> 3.79 us  [program(): f_got = lax.ppermute(f_give, 'c', swap())]
  transfers between devices with their start and end apart: 22 -> 22, of which waited for: 10 -> 11; matrix products, arithmetic and copies ran while one was open for 1% -> 1% of each run, Pallas kernels for 13% -> 14%
where the time goes in v4:
time: 174 us; the launch traced here: 173 us
  blocking collectives  60.4 us (35%)
  waiting for transfers between devices  39.9 us (23%)
  starting transfers between devices  39.6 us (23%)
  Pallas kernels  29.7 us (17%)
  local copies, waits for them, and re-layouts  1.79 us (1%)
    all_to_all x1, blocking collectives, program(): parts = lax.all_to_all(partial_value, CHIPS, 0, 0, tiled=True)  24.6 us
    all_to_all x1, blocking collectives, program(): terms = lax.all_to_all(both, CHIPS, 0, 0, tiled=True)  20.8 us
    pallas_call x4, Pallas kernels, exchange(): pl.pallas_call(make_exchange_kernel([a.shape for a in held], which, first...  20.2 us
    all_to_all x1, blocking collectives, program(): lax.all_to_all(summed.reshape(16, 32, 128), COL, 0, 0, tiled=True)  14.9 us
    ppermute x3, waiting for transfers between devices, program(): up.append(lax.ppermute(up[-1], 'z', ring(8, 1)))  12.4 us
    ppermute x3, starting transfers between devices, program(): down.append(lax.ppermute(down[-1], 'z', ring(8, -1)))  12.1 us
    ppermute x1, waiting for transfers between devices, program(): cols[7] = lax.ppermute(cols[4], 'x', ring(4, -1))  8.1 us
    ppermute x1, waiting for transfers between devices, program(): cols[3] = lax.ppermute(base, 'x', ring(4, -1))  7.3 us
  transfers between devices with their start and end apart: 22, of which 11 were waited for; matrix products, arithmetic and copies ran while one was open for 1% of the time, Pallas kernels for 14%

profile of v4, /device:TPU:1, one launch (start us, length us, event | category | flops | bytes accessed | tf_op | source)
XLA Modules:
  0.0 172.8 jit_solution(6562293115544684978)
XLA Ops:
  0.0 1.1 dynamic-slice_bitcast_fusion
  1.1 3.3 %collective-permute-start = (bf16[8,128,128]{2,1,0:T(8,128)(2,1)S(1)}, bf16[8,128,128]{2,1,0:T(8,128)(2,1)S(1)}, u32[]{:S(2)}, u32[]{:S(2)}) collective-permute-start(bf16[8,128,128]{2,1,0:T(8,128)(2,1)S(1)} %get-tuple-element.33), channel_id=1, source_target_pairs={{0,16},{16,0},{1,17},{17,1},{2,18},{18,2},{3,19},{19,3},{4,20},{20... | collective-permute-start | bytes 786440 | tf_op jit(solution)/shard_map/ppermute | solution.py:255
  4.4 0.9 pad_maximum_fusion.2.stacked
  5.3 0.1 collective-permute-start.1
  5.4 1.4 collective-permute-done.1.other
  6.8 1.3 encode.1
  8.1 24.6 %all_to_all.20.parts = bf16[8,256,384]{2,1,0:T(8,128)(2,1)S(1)} all-to-all(bf16[8,256,384]{2,1,0:T(8,128)(2,1)S(1)} %encode.1), channel_id=1, replica_groups=mesh['yl'=2,'x'=4,'c'=2,'z'=8,'yh'=2] {'yl','x'}, dimensions={0} | all-to-all | bytes 3145728 | tf_op jit(solution)/shard_map/all_to_all | solution.py:258
  32.7 1.0 own.1
  33.8 2.6 %collective-permute-start.2 = (bf16[784,128]{1,0:T(8,128)(2,1)S(1)}, bf16[784,128]{1,0:T(8,128)(2,1)S(1)}, u32[]{:S(2)}, u32[]{:S(2)}) collective-permute-start(bf16[784,128]{1,0:T(8,128)(2,1)S(1)} %get-tuple-element.19), channel_id=1, source_target_pairs={{0,1},{1,0},{2,3},{3,2},{4,5},{5,4},{6,7},{7,6},{8,9},{9,8},{10,11... | collective-permute-start | bytes 602120 | tf_op jit(solution)/shard_map/ppermute | solution.py:261
  36.4 3.5 %all-to-all-start.1 = ((bf16[8,256,128]{2,1,0:T(8,128)(2,1)}), bf16[8,256,128]{2,1,0:T(8,128)(2,1)S(1)}, u32[]{:S(2)}, u32[]{:S(2)}) async-start(bf16[8,256,128]{2,1,0:T(8,128)(2,1)} %get-tuple-element.21), calls=%async_computation.1 | async-start | bytes 1048576 | tf_op jit(solution)/shard_map/all_to_all | solution.py:263
  39.9 1.1 collective-permute-done.2
  41.1 5.7 %collective-permute-start.7 = (bf16[2,784,128]{2,1,0:T(8,128)(2,1)S(1)}, bf16[2,784,128]{2,1,0:T(8,128)(2,1)}, u32[]{:S(2)}, u32[]{:S(2)}) collective-permute-start(bf16[2,784,128]{2,1,0:T(8,128)(2,1)S(1)} %pad_maximum_fusion.1.refs_0_), channel_id=1, source_target_pairs={{0,14},{2,0},{4,2},{6,4},{8,6},{10,8},{12,10},{14,12},{1,15},{3,1}... | collective-permute-start | bytes 1204232 | tf_op jit(solution)/shard_map/ppermute | solution.py:268
  46.8 0.3 collective-permute-start.13
  47.1 3.0 %all-to-all-done.1.refs_4_.refs_3_ = bf16[8,256,128]{2,1,0:T(8,128)(2,1)S(1)} async-done(((bf16[8,256,128]{2,1,0:T(8,128)(2,1)}), bf16[8,256,128]{2,1,0:T(8,128)(2,1)S(1)}, u32[]{:S(2)}, u32[]{:S(2)}) %all-to-all-start.1) | async-done | bytes 524320 | tf_op jit(solution)/shard_map/all_to_all | solution.py:263
  50.1 0.8 collective-permute-start.11
  50.9 2.0 %collective-permute-start.3 = (bf16[2,784,128]{2,1,0:T(8,128)(2,1)S(1)}, bf16[2,784,128]{2,1,0:T(8,128)(2,1)}, u32[]{:S(2)}, u32[]{:S(2)}) collective-permute-start(bf16[2,784,128]{2,1,0:T(8,128)(2,1)S(1)} %pad_maximum_fusion.1.refs_0_), channel_id=1, source_target_pairs={{0,2},{2,4},{4,6},{6,8},{8,10},{10,12},{12,14},{14,0},{1,3},{3,5},... | collective-permute-start | bytes 1204232 | tf_op jit(solution)/shard_map/ppermute | solution.py:267
  52.9 0.2 collective-permute-done.7.refs_2_
  53.1 3.7 %collective-permute-start.8 = (bf16[2,784,128]{2,1,0:T(8,128)(2,1)}, bf16[2,784,128]{2,1,0:T(8,128)(2,1)S(1)}, u32[]{:S(2)}, u32[]{:S(2)}) collective-permute-start(bf16[2,784,128]{2,1,0:T(8,128)(2,1)} %collective-permute-done.7.refs_2_), channel_id=1, source_target_pairs={{0,14},{2,0},{4,2},{6,4},{8,6},{10,8},{12,10},{14,12},{1,15},{3,1}... | collective-permute-start | bytes 1204232 | tf_op jit(solution)/shard_map/ppermute | solution.py:268
  56.8 9.8 %collective-permute-done.3.refs_1_ = bf16[2,784,128]{2,1,0:T(8,128)(2,1)} collective-permute-done((bf16[2,784,128]{2,1,0:T(8,128)(2,1)S(1)}, bf16[2,784,128]{2,1,0:T(8,128)(2,1)}, u32[]{:S(2)}, u32[]{:S(2)}) %collective-permute-start.3) | collective-permute-done | bytes 401440 | tf_op jit(solution)/shard_map/ppermute | solution.py:267
  66.6 0.1 stack.91.pos
  66.7 0.3 collective-permute-start.16
  67.0 4.1 %fetch.1.refs_3_.refs_2_ = bf16[16,128,2048]{2,1,0:T(8,128)(2,1)S(1)} custom-call(s32[19]{0:T(128)S(1)} %stack.91.pos, bf16[16,128,2048]{2,1,0:T(8,128)(2,1)} %kern.1), custom_call_target="tpu_custom_call" | custom-call | flops 1048576 | bytes 8388608 | tf_op jit(solution)/shard_map/fetch/pallas_call | solution.py:77
  71.1 0.3 collective-permute-start.14
  71.4 2.7 %collective-permute-start.9 = (bf16[2,784,128]{2,1,0:T(8,128)(2,1)S(1)}, bf16[2,784,128]{2,1,0:T(8,128)(2,1)S(1)}, u32[]{:S(2)}, u32[]{:S(2)}) collective-permute-start(bf16[2,784,128]{2,1,0:T(8,128)(2,1)S(1)} %collective-permute-done.8.refs_1_), channel_id=1, source_target_pairs={{0,14},{2,0},{4,2},{6,4},{8,6},{10,8},{12,10},{14,12},{1,15},{3,1}... | collective-permute-start | bytes 1204232 | tf_op jit(solution)/shard_map/ppermute | solution.py:268
  74.1 6.5 %exchange.4 = (f32[512,2048]{1,0:T(8,128)S(1)}, f32[16,2048]{1,0:T(8,128)S(1)}) custom-call(s32[19]{0:T(128)S(1)} %stack.91.pos, bf16[2,784,128]{2,1,0:T(8,128)(2,1)S(1)} %pad_maximum_fusion.1.refs_0_, bf16[2,784,128]{2,1,0:T(8,128)(2,1)} %collective-permute-done.3.refs_1_, bf16[2,784,128]{2,1,0:T(8,128)(2,1)} %collective-permute-done.7.refs_2_, ...), custom_call_target="tpu_custom_call" | custom-call | flops 3221225472 | bytes 8388608 | tf_op jit(solution)/shard_map/exchange/pallas_call | solution.py:192
  80.7 0.3 collective-permute-start.5
  80.9 4.9 %exchange.5 = (f32[512,2048]{1,0:T(8,128)S(1)}, f32[16,2048]{1,0:T(8,128)S(1)}) custom-call(s32[19]{0:T(128)S(1)} %stack.91.pos, bf16[2,784,128]{2,1,0:T(8,128)(2,1)S(1)} %collective-permute-done.4.refs_0_, bf16[2,784,128]{2,1,0:T(8,128)(2,1)S(1)} %collective-permute-done.8.refs_1_, ...), custom_call_target="tpu_custom_call", output_to_operand_aliasing={{0}: (6, {}), {1}: (7, {})} | custom-call | flops 2147483648 | bytes 8388608 | tf_op jit(solution)/shard_map/exchange/pallas_call | solution.py:192
  85.9 2.7 %collective-permute-start.10 = (bf16[784,128]{1,0:T(8,128)(2,1)S(1)}, bf16[784,128]{1,0:T(8,128)(2,1)S(1)}, u32[]{:S(2)}, u32[]{:S(2)}) collective-permute-start(bf16[784,128]{1,0:T(8,128)(2,1)S(1)} %slice_bitcast_fusion), channel_id=1, source_target_pairs={{0,14},{2,0},{4,2},{6,4},{8,6},{10,8},{12,10},{14,12},{1,15},{3,1}... | collective-permute-start | bytes 602120 | tf_op jit(solution)/shard_map/ppermute | solution.py:271
  88.6 2.7 %collective-permute-done.5.refs_0_ = bf16[2,784,128]{2,1,0:T(8,128)(2,1)S(1)} collective-permute-done((bf16[2,784,128]{2,1,0:T(8,128)(2,1)S(1)}, bf16[2,784,128]{2,1,0:T(8,128)(2,1)S(1)}, u32[]{:S(2)}, u32[]{:S(2)}) %collective-permute-start.5) | collective-permute-done | bytes 401440 | tf_op jit(solution)/shard_map/ppermute | solution.py:267
  91.3 0.1 collective-permute-start.6
  91.4 4.9 %exchange.6 = (f32[512,2048]{1,0:T(8,128)S(1)}, f32[16,2048]{1,0:T(8,128)S(1)}) custom-call(s32[19]{0:T(128)S(1)} %stack.91.pos, bf16[2,784,128]{2,1,0:T(8,128)(2,1)S(1)} %collective-permute-done.5.refs_0_, bf16[2,784,128]{2,1,0:T(8,128)(2,1)S(1)} %collective-permute-done.9.refs_1_, ...), custom_call_target="tpu_custom_call", output_to_operand_aliasing={{0}: (6, {}), {1}: (7, {})} | custom-call | flops 2147483648 | bytes 8388608 | tf_op jit(solution)/shard_map/exchange/pallas_call | solution.py:192
  96.3 0.9 collective-permute-done.6.refs_0_
  97.1 3.9 %exchange.7 = (bf16[512,1024]{1,0:T(8,128)(2,1)S(1)}, bf16[512,1024]{1,0:T(8,128)(2,1)S(1)}) custom-call(s32[19]{0:T(128)S(1)} %stack.91.pos, bf16[784,128]{1,0:T(8,128)(2,1)S(1)} %collective-permute-done.6.refs_0_, bf16[784,128]{1,0:T(8,128)(2,1)S(1)} %collective-permute-done.10.refs_1_, bf16[16,128,2048]{2,1,0:T(8,128)(2,1)S(1)} %fetch.1.refs_3_.refs_2_, ...), custom_call_target="tpu_custom_call" | custom-call | flops 1073741824 | bytes 8388608 | tf_op jit(solution)/shard_map/exchange/pallas_call | solution.py:192
  101.0 3.8 %collective-permute-start.12 = (bf16[512,1024]{1,0:T(8,128)(2,1)S(1)}, bf16[512,1024]{1,0:T(8,128)(2,1)S(1)}, u32[]{:S(2)}, u32[]{:S(2)}) collective-permute-start(bf16[512,1024]{1,0:T(8,128)(2,1)S(1)} %get-tuple-element.29), channel_id=1, source_target_pairs={{0,16},{16,0},{1,17},{17,1},{2,18},{18,2},{3,19},{19,3},{4,20},{20... | collective-permute-start | bytes 3145736 | tf_op jit(solution)/shard_map/ppermute | solution.py:289
  104.8 2.4 %collective-permute-start.15 = (bf16[2,1024,128]{2,1,0:T(8,128)(2,1)S(1)}, bf16[2,1024,128]{2,1,0:T(8,128)(2,1)S(1)}, u32[]{:S(2)}, u32[]{:S(2)}) collective-permute-start(bf16[2,1024,128]{2,1,0:T(8,128)(2,1)S(1)} %pad_maximum_fusion.refs_0_), channel_id=1, source_target_pairs={{0,96},{32,0},{64,32},{96,64},{1,97},{33,1},{65,33},{97,65},{2,98}... | collective-permute-start | bytes 1572872 | tf_op jit(solution)/shard_map/ppermute | solution.py:278
  107.3 2.7 %collective-permute-start.19 = (bf16[2,1024,128]{2,1,0:T(8,128)(2,1)S(1)}, bf16[2,1024,128]{2,1,0:T(8,128)(2,1)S(1)}, u32[]{:S(2)}, u32[]{:S(2)}) collective-permute-start(bf16[2,1024,128]{2,1,0:T(8,128)(2,1)S(1)} %collective-permute-done.16.refs_4_), channel_id=1, source_target_pairs={{0,96},{32,0},{64,32},{96,64},{1,97},{33,1},{65,33},{97,65},{2,98}... | collective-permute-start | bytes 1572872 | tf_op jit(solution)/shard_map/ppermute | solution.py:280
  109.9 1.2 collective-permute-start.18
  111.2 7.3 %collective-permute-done.15.refs_3_ = bf16[2,1024,128]{2,1,0:T(8,128)(2,1)S(1)} collective-permute-done((bf16[2,1024,128]{2,1,0:T(8,128)(2,1)S(1)}, bf16[2,1024,128]{2,1,0:T(8,128)(2,1)S(1)}, u32[]{:S(2)}, u32[]{:S(2)}) %collective-permute-start.15) | collective-permute-done | bytes 524320 | tf_op jit(solution)/shard_map/ppermute | solution.py:278
  118.4 3.1 %collective-permute-done.17.refs_5_ = bf16[2,1024,128]{2,1,0:T(8,128)(2,1)S(1)} collective-permute-done((bf16[2,1024,128]{2,1,0:T(8,128)(2,1)S(1)}, bf16[2,1024,128]{2,1,0:T(8,128)(2,1)S(1)}, u32[]{:S(2)}, u32[]{:S(2)}) %collective-permute-start.17) | collective-permute-done | bytes 524320 | tf_op jit(solution)/shard_map/ppermute | solution.py:281
  121.6 8.1 %collective-permute-done.19.refs_7_ = bf16[2,1024,128]{2,1,0:T(8,128)(2,1)S(1)} collective-permute-done((bf16[2,1024,128]{2,1,0:T(8,128)(2,1)S(1)}, bf16[2,1024,128]{2,1,0:T(8,128)(2,1)S(1)}, u32[]{:S(2)}, u32[]{:S(2)}) %collective-permute-start.19) | collective-permute-done | bytes 524320 | tf_op jit(solution)/shard_map/ppermute | solution.py:280
  129.7 3.0 %decode.1 = (bf16[8,512,128]{2,1,0:T(8,128)(2,1)S(1)}, bf16[8,512,128]{2,1,0:T(8,128)(2,1)S(1)}) custom-call(s32[19]{0:T(128)S(1)} %stack.91.pos, bf16[512,1024]{1,0:T(8,128)(2,1)S(1)} %get-tuple-element.28.f_mine, bf16[512,1024]{1,0:T(8,128)(2,1)S(1)} %collective-permute-done.12.f_got, bf16[2,1024,128]{2,1,0:T(8,128)(2,1)S(1)} %pad_maximum_fusion.refs_0_, ...), custom_call_target="tpu_custom_call" | custom-call | flops 2147483648 | bytes 8388608 | tf_op jit(solution)/shard_map/decode/pallas_call | solution.py:216
  132.7 1.0 collective-permute-start.20
  133.7 2.3 %collective-permute-done.20 = bf16[8,512,128]{2,1,0:T(8,128)(2,1)S(1)} collective-permute-done((bf16[8,512,128]{2,1,0:T(8,128)(2,1)S(1)}, bf16[8,512,128]{2,1,0:T(8,128)(2,1)S(1)}, u32[]{:S(2)}, u32[]{:S(2)}) %collective-permute-start.20) | collective-permute-done | bytes 1048608 | tf_op jit(solution)/shard_map/ppermute | solution.py:291
  136.0 0.3 add_convert_fusion
  136.3 20.8 %all_to_all.21.parts = bf16[8,512,128]{2,1,0:T(8,128)(2,1)S(1)} all-to-all(bf16[8,512,128]{2,1,0:T(8,128)(2,1)S(1)} %add_convert_fusion), channel_id=1, replica_groups=mesh['yl'=2,'x'=4,'c'=2,'z'=8,'yh'=2] {'yl','x'}, dimensions={0} | all-to-all | bytes 2097152 | tf_op jit(solution)/shard_map/all_to_all | solution.py:293
  157.1 0.1 chip_sum.1
  157.3 14.9 %all_to_all.22 = bf16[16,32,128]{2,1,0:T(8,128)(2,1)S(1)} all-to-all(bf16[16,32,128]{2,1,0:T(8,128)(2,1)S(1)} %bitcast.44), channel_id=1, replica_groups=mesh['yl'=2,'x'=4,'c'=2,'z'=8,'yh'=2] {'z','yh'}, dimensions={0} | all-to-all | bytes 262144 | tf_op jit(solution)/shard_map/all_to_all | solution.py:302
  172.2 0.6 copy.13
  (19 shorter events, 0.2 us)
Async XLA Ops:
  1.1 5.7 %collective-permute-start = (bf16[8,128,128]{2,1,0:T(8,128)(2,1)S(1)}, bf16[8,128,128]{2,1,0:T(8,128)(2,1)S(1)}, u32[]{:S(2)}, u32[]{:S(2)}) collective-permute-start(bf16[8,128,128]{2,1,0:T(8,128)(2,1)S(1)} %get-tuple-element.33), channel_id=1, source_target_pairs={{0,16},{16,0},{1,17},{17,1},{2,18},{18,2},{3,19},{19,3},{4,20},{20... | collective-permute-start | bytes 786440 | tf_op jit(solution)/shard_map/ppermute | solution.py:255
  5.3 1.5 collective-permute-start.1
  33.8 7.2 %collective-permute-start.2 = (bf16[784,128]{1,0:T(8,128)(2,1)S(1)}, bf16[784,128]{1,0:T(8,128)(2,1)S(1)}, u32[]{:S(2)}, u32[]{:S(2)}) collective-permute-start(bf16[784,128]{1,0:T(8,128)(2,1)S(1)} %get-tuple-element.19), channel_id=1, source_target_pairs={{0,1},{1,0},{2,3},{3,2},{4,5},{5,4},{6,7},{7,6},{8,9},{9,8},{10,11... | collective-permute-start | bytes 602120 | tf_op jit(solution)/shard_map/ppermute | solution.py:261
  36.4 13.7 %all-to-all-start.1 = ((bf16[8,256,128]{2,1,0:T(8,128)(2,1)}), bf16[8,256,128]{2,1,0:T(8,128)(2,1)S(1)}, u32[]{:S(2)}, u32[]{:S(2)}) async-start(bf16[8,256,128]{2,1,0:T(8,128)(2,1)} %get-tuple-element.21), calls=%async_computation.1 | async-start | bytes 1048576 | tf_op jit(solution)/shard_map/all_to_all | solution.py:263
  41.1 12.0 %collective-permute-start.7 = (bf16[2,784,128]{2,1,0:T(8,128)(2,1)S(1)}, bf16[2,784,128]{2,1,0:T(8,128)(2,1)}, u32[]{:S(2)}, u32[]{:S(2)}) collective-permute-start(bf16[2,784,128]{2,1,0:T(8,128)(2,1)S(1)} %pad_maximum_fusion.1.refs_0_), channel_id=1, source_target_pairs={{0,14},{2,0},{4,2},{6,4},{8,6},{10,8},{12,10},{14,12},{1,15},{3,1}... | collective-permute-start | bytes 1204232 | tf_op jit(solution)/shard_map/ppermute | solution.py:268
  46.8 24.3 %collective-permute-start.13 = (bf16[2,1024,128]{2,1,0:T(8,128)(2,1)S(1)}, bf16[2,1024,128]{2,1,0:T(8,128)(2,1)S(1)}, u32[]{:S(2)}, u32[]{:S(2)}) collective-permute-start(bf16[2,1024,128]{2,1,0:T(8,128)(2,1)S(1)} %pad_maximum_fusion.refs_0_), channel_id=1, source_target_pairs={{0,32},{32,64},{64,96},{96,0},{1,33},{33,65},{65,97},{97,1},{2,34}... | collective-permute-start | bytes 1572872 | tf_op jit(solution)/shard_map/ppermute | solution.py:277
  50.1 24.0 %collective-permute-start.11 = (bf16[8,256,128]{2,1,0:T(8,128)(2,1)S(1)}, bf16[8,256,128]{2,1,0:T(8,128)(2,1)S(1)}, u32[]{:S(2)}, u32[]{:S(2)}) collective-permute-start(bf16[8,256,128]{2,1,0:T(8,128)(2,1)S(1)} %all-to-all-done.1.refs_4_.refs_3_), channel_id=1, source_target_pairs={{0,16},{16,0},{1,17},{17,1},{2,18},{18,2},{3,19},{19,3},{4,20},{20... | collective-permute-start | bytes 1572872 | tf_op jit(solution)/shard_map/ppermute | solution.py:264
  50.9 15.7 %collective-permute-start.3 = (bf16[2,784,128]{2,1,0:T(8,128)(2,1)S(1)}, bf16[2,784,128]{2,1,0:T(8,128)(2,1)}, u32[]{:S(2)}, u32[]{:S(2)}) collective-permute-start(bf16[2,784,128]{2,1,0:T(8,128)(2,1)S(1)} %pad_maximum_fusion.1.refs_0_), channel_id=1, source_target_pairs={{0,2},{2,4},{4,6},{6,8},{8,10},{10,12},{12,14},{14,0},{1,3},{3,5},... | collective-permute-start | bytes 1204232 | tf_op jit(solution)/shard_map/ppermute | solution.py:267
  53.1 18.3 %collective-permute-start.8 = (bf16[2,784,128]{2,1,0:T(8,128)(2,1)}, bf16[2,784,128]{2,1,0:T(8,128)(2,1)S(1)}, u32[]{:S(2)}, u32[]{:S(2)}) collective-permute-start(bf16[2,784,128]{2,1,0:T(8,128)(2,1)} %collective-permute-done.7.refs_2_), channel_id=1, source_target_pairs={{0,14},{2,0},{4,2},{6,4},{8,6},{10,8},{12,10},{14,12},{1,15},{3,1}... | collective-permute-start | bytes 1204232 | tf_op jit(solution)/shard_map/ppermute | solution.py:268
  66.6 14.1 %collective-permute-start.4 = (bf16[2,784,128]{2,1,0:T(8,128)(2,1)}, bf16[2,784,128]{2,1,0:T(8,128)(2,1)S(1)}, u32[]{:S(2)}, u32[]{:S(2)}) collective-permute-start(bf16[2,784,128]{2,1,0:T(8,128)(2,1)} %collective-permute-done.3.refs_1_), channel_id=1, source_target_pairs={{0,2},{2,4},{4,6},{6,8},{8,10},{10,12},{12,14},{14,0},{1,3},{3,5},... | collective-permute-start | bytes 1204232 | tf_op jit(solution)/shard_map/ppermute | solution.py:267
  66.7 40.6 %collective-permute-start.16 = (bf16[2,1024,128]{2,1,0:T(8,128)(2,1)S(1)}, bf16[2,1024,128]{2,1,0:T(8,128)(2,1)S(1)}, u32[]{:S(2)}, u32[]{:S(2)}) collective-permute-start(bf16[2,1024,128]{2,1,0:T(8,128)(2,1)S(1)} %pad_maximum_fusion.refs_0_), channel_id=1, source_target_pairs={{0,128},{128,0},{1,129},{129,1},{2,130},{130,2},{3,131},{131,3},{4... | collective-permute-start | bytes 1572872 | tf_op jit(solution)/shard_map/ppermute | solution.py:276
  71.1 38.8 %collective-permute-start.14 = (bf16[2,1024,128]{2,1,0:T(8,128)(2,1)S(1)}, bf16[2,1024,128]{2,1,0:T(8,128)(2,1)S(1)}, u32[]{:S(2)}, u32[]{:S(2)}) collective-permute-start(bf16[2,1024,128]{2,1,0:T(8,128)(2,1)S(1)} %collective-permute-done.13.refs_1_), channel_id=1, source_target_pairs={{0,32},{32,64},{64,96},{96,0},{1,33},{33,65},{65,97},{97,1},{2,34}... | collective-permute-start | bytes 1572872 | tf_op jit(solution)/shard_map/ppermute | solution.py:279
  71.4 14.4 %collective-permute-start.9 = (bf16[2,784,128]{2,1,0:T(8,128)(2,1)S(1)}, bf16[2,784,128]{2,1,0:T(8,128)(2,1)S(1)}, u32[]{:S(2)}, u32[]{:S(2)}) collective-permute-start(bf16[2,784,128]{2,1,0:T(8,128)(2,1)S(1)} %collective-permute-done.8.refs_1_), channel_id=1, source_target_pairs={{0,14},{2,0},{4,2},{6,4},{8,6},{10,8},{12,10},{14,12},{1,15},{3,1}... | collective-permute-start | bytes 1204232 | tf_op jit(solution)/shard_map/ppermute | solution.py:268
  80.7 10.6 %collective-permute-start.5 = (bf16[2,784,128]{2,1,0:T(8,128)(2,1)S(1)}, bf16[2,784,128]{2,1,0:T(8,128)(2,1)S(1)}, u32[]{:S(2)}, u32[]{:S(2)}) collective-permute-start(bf16[2,784,128]{2,1,0:T(8,128)(2,1)S(1)} %collective-permute-done.4.refs_0_), channel_id=1, source_target_pairs={{0,2},{2,4},{4,6},{6,8},{8,10},{10,12},{12,14},{14,0},{1,3},{3,5},... | collective-permute-start | bytes 1204232 | tf_op jit(solution)/shard_map/ppermute | solution.py:267
  85.9 10.4 %collective-permute-start.10 = (bf16[784,128]{1,0:T(8,128)(2,1)S(1)}, bf16[784,128]{1,0:T(8,128)(2,1)S(1)}, u32[]{:S(2)}, u32[]{:S(2)}) collective-permute-start(bf16[784,128]{1,0:T(8,128)(2,1)S(1)} %slice_bitcast_fusion), channel_id=1, source_target_pairs={{0,14},{2,0},{4,2},{6,4},{8,6},{10,8},{12,10},{14,12},{1,15},{3,1}... | collective-permute-start | bytes 602120 | tf_op jit(solution)/shard_map/ppermute | solution.py:271
  91.3 5.9 %collective-permute-start.6 = (bf16[784,128]{1,0:T(8,128)(2,1)S(1)}, bf16[784,128]{1,0:T(8,128)(2,1)S(1)}, u32[]{:S(2)}, u32[]{:S(2)}) collective-permute-start(bf16[784,128]{1,0:T(8,128)(2,1)S(1)} %slice_bitcast_fusion.1), channel_id=1, source_target_pairs={{0,2},{2,4},{4,6},{6,8},{8,10},{10,12},{12,14},{14,0},{1,3},{3,5},... | collective-permute-start | bytes 602120 | tf_op jit(solution)/shard_map/ppermute | solution.py:270
  101.0 28.7 %collective-permute-start.12 = (bf16[512,1024]{1,0:T(8,128)(2,1)S(1)}, bf16[512,1024]{1,0:T(8,128)(2,1)S(1)}, u32[]{:S(2)}, u32[]{:S(2)}) collective-permute-start(bf16[512,1024]{1,0:T(8,128)(2,1)S(1)} %get-tuple-element.29), channel_id=1, source_target_pairs={{0,16},{16,0},{1,17},{17,1},{2,18},{18,2},{3,19},{19,3},{4,20},{20... | collective-permute-start | bytes 3145736 | tf_op jit(solution)/shard_map/ppermute | solution.py:289
  104.8 13.6 %collective-permute-start.15 = (bf16[2,1024,128]{2,1,0:T(8,128)(2,1)S(1)}, bf16[2,1024,128]{2,1,0:T(8,128)(2,1)S(1)}, u32[]{:S(2)}, u32[]{:S(2)}) collective-permute-start(bf16[2,1024,128]{2,1,0:T(8,128)(2,1)S(1)} %pad_maximum_fusion.refs_0_), channel_id=1, source_target_pairs={{0,96},{32,0},{64,32},{96,64},{1,97},{33,1},{65,33},{97,65},{2,98}... | collective-permute-start | bytes 1572872 | tf_op jit(solution)/shard_map/ppermute | solution.py:278
  107.3 14.3 %collective-permute-start.17 = (bf16[2,1024,128]{2,1,0:T(8,128)(2,1)S(1)}, bf16[2,1024,128]{2,1,0:T(8,128)(2,1)S(1)}, u32[]{:S(2)}, u32[]{:S(2)}) collective-permute-start(bf16[2,1024,128]{2,1,0:T(8,128)(2,1)S(1)} %collective-permute-done.16.refs_4_), channel_id=1, source_target_pairs={{0,32},{32,64},{64,96},{96,0},{1,33},{33,65},{65,97},{97,1},{2,34}... | collective-permute-start | bytes 1572872 | tf_op jit(solution)/shard_map/ppermute | solution.py:281
  107.3 22.4 %collective-permute-start.19 = (bf16[2,1024,128]{2,1,0:T(8,128)(2,1)S(1)}, bf16[2,1024,128]{2,1,0:T(8,128)(2,1)S(1)}, u32[]{:S(2)}, u32[]{:S(2)}) collective-permute-start(bf16[2,1024,128]{2,1,0:T(8,128)(2,1)S(1)} %collective-permute-done.16.refs_4_), channel_id=1, source_target_pairs={{0,96},{32,0},{64,32},{96,64},{1,97},{33,1},{65,33},{97,65},{2,98}... | collective-permute-start | bytes 1572872 | tf_op jit(solution)/shard_map/ppermute | solution.py:280
  109.9 19.7 %collective-permute-start.18 = (bf16[2,1024,128]{2,1,0:T(8,128)(2,1)S(1)}, bf16[2,1024,128]{2,1,0:T(8,128)(2,1)S(1)}, u32[]{:S(2)}, u32[]{:S(2)}) collective-permute-start(bf16[2,1024,128]{2,1,0:T(8,128)(2,1)S(1)} %collective-permute-done.14.refs_2_), channel_id=1, source_target_pairs={{0,128},{128,0},{1,129},{129,1},{2,130},{130,2},{3,131},{131,3},{4... | collective-permute-start | bytes 1572872 | tf_op jit(solution)/shard_map/ppermute | solution.py:282
  132.7 3.3 %collective-permute-start.20 = (bf16[8,512,128]{2,1,0:T(8,128)(2,1)S(1)}, bf16[8,512,128]{2,1,0:T(8,128)(2,1)S(1)}, u32[]{:S(2)}, u32[]{:S(2)}) collective-permute-start(bf16[8,512,128]{2,1,0:T(8,128)(2,1)S(1)} %get-tuple-element.32), channel_id=1, source_target_pairs={{0,16},{16,0},{1,17},{17,1},{2,18},{18,2},{3,19},{19,3},{4,20},{20... | collective-permute-start | bytes 3145736 | tf_op jit(solution)/shard_map/ppermute | solution.py:291
